TPU v7x, 1024 devices: a whole 4x4x32 slice. The times are simulated.
1024 devices in a mesh: dp: 64 (over z_lo, x), expert: 16 (over y, z_hi, core).
Axes of the slice: x: 4, y: 4, z: 32 (z_hi: 2, z_lo: 16; z = z_hi * 16 + z_lo), core: 2. Of those that a mesh axis runs over, the one named last changes fastest.
Arguments:
- out_grad: bfloat16 [1024, 3072], P('expert', 'dp'), may hold values from -6 to 6
- gate_probs: bfloat16 [1024, 2], P('expert'), may hold values from 0.049804688 to 1
- expert_ids: int32 [1024, 2], P('expert'), may hold values from 0 to 7, all different within a row; in each aligned block of 64 rows (0 to 63, 64 to 127, ...) at most 20 rows name the same one
- saved_gate: bfloat16 [16, 320, 8192], P('expert', None, 'dp'), may hold values from -8 to 8
- saved_up: bfloat16 [16, 320, 8192], P('expert', None, 'dp'), may hold values from -6 to 6
- w_gate: bfloat16 [16, 3072, 8192], P('expert', None, 'dp'), may hold values from -0.109375 to 0.109375
- w_up: bfloat16 [16, 3072, 8192], P('expert', None, 'dp'), may hold values from -0.109375 to 0.109375
- w_down: bfloat16 [16, 8192, 3072], P('expert', 'dp'), may hold values from -0.046875 to 0.046875
Outputs:
- token_grads: bfloat16 [1024, 3072], P('expert', 'dp')
Inputs may be any that keep to these rules, and one draw needn't show every extreme that they name: `expert_ids`: the 2 ids of a row differ. Within the rows of one device (aligned blocks of 64 rows) no expert is named by more than 20 rows, a bound that some block reaches.
All inputs are finite; a program needn't handle non-finite values.
Results may differ from a plain program's by a relative error of at most 0.013.
Values may be sent and summed in bfloat16 or wider, within the bound.
No kernel may reach another device: no remote copies, remote signals or barrier semaphores. Data moves between devices by JAX's collectives and lax.ppermute only.
A program may use at most 32 MiB of HBM per device.

v0:
```python
import jax
import jax.numpy as jnp
from jax import lax
from jax.sharding import Mesh
from jax.sharding import PartitionSpec as P

SPLIT = 2
EXPERT = ("expert_0", "expert_1", "expert_2")
DP = ("dp_0", "dp_1")


def in_one_piece(arrays, axis, split_dim, concat_dim, along):
    columns = [a.reshape(*a.shape[:along], -1) for a in arrays]
    both = jnp.concatenate(columns, axis=along)
    result, at, done = (
        lax.all_to_all(both, axis, split_axis=split_dim, concat_axis=concat_dim, tiled=True),
        0,
        [],
    )
    for a, column in zip(arrays, columns):
        piece = result[..., at : at + column.shape[along]]
        done.append(piece.reshape(*piece.shape[:along], *a.shape[along:]))
        at += column.shape[along]
    return tuple(done)


def in_order(tiles, dim):
    dims = list(tiles.shape[1:])
    dims[dim] *= tiles.shape[0]
    return jnp.moveaxis(tiles, 0, dim).reshape(dims)


def gather_in_order(value, axes, sequence):
    tiles = value
    for k in sequence:
        tiles = lax.all_gather(tiles, axes[k])
    done = sequence[::-1]
    back = [done.index(k) for k in range(len(axes))]
    tiles = tiles.transpose(*back, *range(len(axes), tiles.ndim))
    return tiles.reshape(-1, *value.shape)


def gather_axes(value, axes, sequence, dim):
    return in_order(gather_in_order(value, axes, sequence), dim)


def own_block(tiles, axes, sequence):
    dims = [lax.axis_size(a) for a in axes]
    tiles = tiles.reshape(*dims, *tiles.shape[1:])
    tiles = tiles.transpose(*sequence, *range(len(axes), tiles.ndim))
    tiles = tiles.reshape(-1, *tiles.shape[len(axes) :])
    for k in sequence:
        tiles = lax.psum_scatter(tiles, axes[k], scatter_dimension=0, tiled=True)
    return tiles[0]


def cut_along(value, dim, peers):
    dims = value.shape
    tiles = value.reshape(*dims[:dim], peers, dims[dim] // peers, *dims[dim + 1 :])
    return jnp.moveaxis(tiles, dim, 0)


def summed_rows_2(value, axes, sequence, dim):
    peers = lax.axis_size(axes)
    return own_block(cut_along(value, dim, peers), axes, sequence)


def exchange_in_order(tiles, axes, sequence):
    dims = [lax.axis_size(a) for a in axes]
    tiles = tiles.reshape(*dims, *tiles.shape[1:])
    for k in sequence:
        tiles = lax.all_to_all(tiles, axes[k], split_axis=k, concat_axis=k, tiled=True)
    return tiles.reshape(-1, *tiles.shape[len(axes) :])


def core_and_chips(value, groups, sequence, split_dim, concat_dim):
    peers = lax.axis_size(groups[0]) * lax.axis_size(groups[1])
    tiles = cut_along(value, split_dim, peers)
    return in_order(exchange_in_order(tiles, groups, sequence), concat_dim)


def local(out_grad, gate_probs, expert_ids, saved_gate, saved_up, w_gate, w_up, w_down):
    groups = lax.axis_size(EXPERT)
    experts = groups // SPLIT
    columns = out_grad.shape[1]
    tok_rows = out_grad.shape[0]
    slot_count = saved_gate.shape[1]
    capacity = slot_count // groups
    experts_iota = jnp.arange(experts, dtype=jnp.int32)
    chosen = (expert_ids[:, :, None] == experts_iota[None, None, :]).astype(jnp.int32)
    per_token = jnp.sum(chosen, axis=1, dtype=jnp.int32)
    ranked = jnp.cumsum(per_token, axis=0, dtype=jnp.int32) - per_token
    position = jnp.sum(chosen * ranked[:, None, :], axis=2, dtype=jnp.int32)
    target = expert_ids * capacity + position
    slot_iota = jnp.arange(experts * capacity, dtype=jnp.int32)
    matches = slot_iota[:, None, None] == target[None, :, :]
    picker = jnp.any(matches, axis=2).astype(jnp.bfloat16)
    picker = jnp.repeat(picker.reshape(experts, capacity, tok_rows), SPLIT, axis=0).reshape(
        groups * capacity, tok_rows
    )
    weighted = jnp.where(matches, gate_probs.astype(jnp.float32)[None, :, :], 0.0)
    prob_slots = jnp.sum(weighted, axis=(1, 2)).astype(jnp.bfloat16).reshape(experts, capacity)
    prob_slots = jnp.repeat(prob_slots, SPLIT, axis=0)
    down_here = w_down[0]
    dispatched = jnp.dot(picker, out_grad, preferred_element_type=jnp.float32).astype(jnp.bfloat16)
    arrived, arrived_probs = in_one_piece(
        (dispatched.reshape(groups, capacity, columns), prob_slots), EXPERT, 0, 0, 2
    )
    projected = lax.dot_general(
        gather_axes(arrived.reshape(slot_count, columns), DP, (0, 1), 1),
        down_here,
        (((1,), (1,)), ((), ())),
        preferred_element_type=jnp.float32,
    )
    gate_pre = saved_gate[0].astype(jnp.float32)
    up_pre = saved_up[0].astype(jnp.float32)
    sigmoid_gate = jax.nn.sigmoid(gate_pre)
    hidden_grad = arrived_probs.reshape(slot_count).astype(jnp.float32)[:, None] * projected
    gate_grad = (
        hidden_grad * up_pre * sigmoid_gate * (1.0 + gate_pre * (1.0 - sigmoid_gate))
    ).astype(jnp.bfloat16)
    up_grad = (hidden_grad * gate_pre * sigmoid_gate).astype(jnp.bfloat16)
    gate_here = w_gate[0]
    up_here = w_up[0]
    first = lax.dot_general(
        gate_here, gate_grad, (((1,), (1,)), ((), ())), preferred_element_type=jnp.float32
    )
    second = lax.dot_general(
        up_here, up_grad, (((1,), (1,)), ((), ())), preferred_element_type=jnp.float32
    )
    shares = summed_rows_2(first + second, DP, (1, 0), 0)
    returned = core_and_chips(
        shares.astype(jnp.bfloat16).reshape(columns, groups, capacity),
        (("expert_0", "expert_1"), "expert_2"),
        (1, 0),
        1,
        1,
    )
    summed = jnp.dot(
        returned.reshape(columns, groups * capacity), picker, preferred_element_type=jnp.float32
    )
    return summed.T.astype(jnp.bfloat16)


def solution(mesh):
    split = Mesh(
        mesh.devices.reshape(16, 4, 4, 2, 2), ("dp_0", "dp_1", "expert_0", "expert_1", "expert_2")
    )
    return jax.shard_map(
        local,
        mesh=split,
        in_specs=(
            P(EXPERT, DP),
            P(EXPERT, None),
            P(EXPERT, None),
            P(EXPERT, None, DP),
            P(EXPERT, None, DP),
            P(EXPERT, None, DP),
            P(EXPERT, None, DP),
            P(EXPERT, DP, None),
        ),
        out_specs=P(EXPERT, DP),
        check_vma=False,
    )
```

profile of v0, /device:TPU:6, one launch (start us, length us, event | category | flops | bytes accessed | tf_op | source)
XLA Modules:
  0.0 535.5 jit_solution(10868685782316448363)
XLA Ops:
  6.5 0.7 convert_element_type.71
  7.3 0.7 convert_reduce_fusion.1
  8.0 0.1 copy.54
  8.0 0.1 reduce_window_sum.11
  8.1 0.1 copy.56
  8.2 0.7 select_reduce_fusion.1
  8.9 0.7 multiply_add_fusion
  9.6 0.1 fusion.14
  9.7 0.1 select_reduce_fusion
  9.8 0.1 convert_element_type.73
  9.9 0.1 copy.57
  10.1 0.0 copy-start.2
  10.1 0.9 convolution_convert_fusion
  11.1 0.1 copy.58
  11.2 0.2 copy.59
  11.5 0.1 pad_maximum_fusion
  11.6 0.1 reshape.71
  11.7 55.3 %all_to_all.15 = bf16[16,2,490]{2,1,0:T(2,128)(2,1)S(1)} all-to-all(bf16[16,2,490]{2,1,0:T(2,128)(2,1)S(1)} %reshape.71), channel_id=1, replica_groups=mesh['dp_0'=16,'dp_1'=4,'expert_0'=4,'expert_1'=2,'expert_2'=2] {'expert..., dimensions={0} | all-to-all | bytes 62720 | tf_op jit(solution)/shard_map/all_to_all | solution.py:16
  67.0 0.1 reshape.72
  67.2 0.1 copy.60
  67.3 101.0 %all_gather.9 = bf16[16,320,48]{1,2,0:T(8,128)(2,1)} all-gather(bf16[1,320,48]{1,2,0:T(8,128)(2,1)S(1)} %copy.60), channel_id=1, replica_groups=mesh['dp_0'=16,'dp_1'=4,'expert_0'=4,'expert_1'=2,'expert_2'=2] {'dp_0'}, dimensions={0}, use_global_device_ids=true | all-gather | bytes 522240 | tf_op jit(solution)/shard_map/all_gather | solution.py:36
  168.3 0.0 all-gather.3.cloned.1.call-update
  168.3 0.0 reduce-scatter.3.cloned.1.call-start
  168.3 0.2 convert_reduce_fusion
  168.6 0.1 reshape.66
  168.6 27.4 %all-gather.3.cloned.1.call-done = bf16[64,320,48]{1,2,0:T(8,128)(2,1)} async-done(((bf16[16,320,48]{1,2,0:T(8,128)(2,1)}), bf16[64,320,48]{1,2,0:T(8,128)(2,1)}) %all-gather.3.cloned.1.call-update) | async-done | bytes 1966096 | tf_op jit(solution)/shard_map/all_gather | solution.py:36
  196.1 2.1 copy.61
  198.2 0.8 convolution_multiply_fusion
  199.0 0.7 fusion.2
  199.7 2.6 fusion
  202.3 5.7 %copy.62 = f32[3072,320]{1,0:T(8,128)} copy(f32[3072,320]{0,1:T(8,128)} %fusion) | data formatting | bytes 7864320 | tf_op jit(solution)/shard_map/add | solution.py:131
  208.0 4.9 copy.63
  212.9 0.0 reduce-scatter.3.cloned.1.call-update
  212.9 0.0 reduce-scatter.5.cloned.1.call-start
  213.0 69.4 %reduce-scatter.3.cloned.1.call-done = f32[16,48,320]{2,1,0:T(8,128)} async-done(((f32[64,48,320]{2,1,0:T(8,128)}), f32[16,48,320]{2,1,0:T(8,128)}) %reduce-scatter.3.cloned.1.call-update) | async-done | bytes 983056 | tf_op jit(solution)/shard_map/reduce_scatter | solution.py:53
  282.4 0.0 reduce-scatter.5.cloned.1.call-update
  282.4 208.2 %reduce-scatter.5.cloned.1.call-done = f32[1,48,320]{2,1,0:T(8,128)} async-done(((f32[16,48,320]{2,1,0:T(8,128)}), f32[1,48,320]{2,1,0:T(8,128)}) %reduce-scatter.5.cloned.1.call-update) | async-done | bytes 61456 | tf_op jit(solution)/shard_map/reduce_scatter | solution.py:53
  490.6 0.9 convert_element_type.82
  491.5 0.1 copy.64
  491.7 0.1 reshape.73
  491.8 3.7 all_to_all.16
  495.6 0.1 reshape.74
  495.7 0.1 copy.71
  495.8 0.1 reshape.75
  495.9 32.0 %all_to_all.17 = bf16[8,2,960]{2,1,0:T(2,128)(2,1)S(1)} all-to-all(bf16[8,2,960]{2,1,0:T(2,128)(2,1)S(1)} %reshape.75), channel_id=1, replica_groups=mesh['dp_0'=16,'dp_1'=4,'expert_0'=4,'expert_1'=2,'expert_2'=2] {'expert..., dimensions={0} | all-to-all | bytes 61440 | tf_op jit(solution)/shard_map/all_to_all | solution.py:72
  527.9 0.1 reshape.76
  528.1 0.1 copy.67
  528.2 0.8 convolution_convert_fusion.1
  (22 shorter events, 0.3 us)
Async XLA Ops:
  6.5 192.4 %copy-start = (bf16[1,3072,128]{2,1,0:T(8,128)(2,1)S(1)}, bf16[1,3072,128]{2,1,0:T(8,128)(2,1)}, u32[]{:S(2)}) copy-start(bf16[1,3072,128]{2,1,0:T(8,128)(2,1)} %param.13) | copy-start | bytes 2359300
  6.5 189.5 %all-gather.3.cloned.1.call-start = ((), (), s32[]{:S(2)}) async-start(), calls=%async_computation.7 | async-start | bytes 2949120 | tf_op jit(solution)/shard_map/all_gather | solution.py:36
  10.1 188.1 %copy-start.2 = (bf16[1,128,3072]{2,1,0:T(8,128)(2,1)S(1)}, bf16[1,128,3072]{2,1,0:T(8,128)(2,1)}, u32[]{:S(2)}) copy-start(bf16[1,128,3072]{2,1,0:T(8,128)(2,1)} %param.15) | copy-start | bytes 2359300
  168.3 114.1 %reduce-scatter.3.cloned.1.call-start = ((), (), s32[]{:S(2)}) async-start(), calls=%async_computation.5 | async-start | bytes 5898240 | tf_op jit(solution)/shard_map/reduce_scatter | solution.py:53
  196.1 2.9 copy-start.3
  196.1 2.9 copy-start.4
  198.1 1.6 copy-start.1
  212.9 277.7 %reduce-scatter.5.cloned.1.call-start = ((), (), s32[]{:S(2)}) async-start(), calls=%async_computation.6 | async-start | bytes 1253376 | tf_op jit(solution)/shard_map/reduce_scatter | solution.py:53
Sparse Core Ops, SparseCore 0:
  168.4 27.5 all-gather.2
  213.0 69.2 reduce-scatter.2
  285.8 204.7 reduce-scatter.4
where the time goes:
time: 536 us
  waiting for transfers between devices  305 us (57%)
  blocking collectives  192 us (36%)
  local copies, waits for them, and re-layouts  14.9 us (3%)
  between operations  13.3 us (2%)
  matrix products  5.81 us (1%)
    reduce_scatter x2, waiting for transfers between devices, own_block(): tiles = lax.psum_scatter(tiles, axes[k], scatter_dimension=0, tiled=True)  278 us
    all_gather x1, blocking collectives, gather_in_order(): tiles = lax.all_gather(tiles, axes[k])  101 us
    all_to_all x1, blocking collectives, in_one_piece(): lax.all_to_all(both, axis, split_axis=split_dim, concat_axis=concat_dim,...  55.3 us
    all_to_all x2, blocking collectives, exchange_in_order(): lax.all_to_all(tiles, axes[k], split_axis=k, concat_axis=k, tiled=True)  35.7 us
    all_gather x1, waiting for transfers between devices, gather_in_order(): tiles = lax.all_gather(tiles, axes[k])  27.4 us
  transfers between devices with their start and end apart: 3, of which 3 were waited for; matrix products, arithmetic and copies ran while one was open for 0% of the time, Pallas kernels for 0%

commit v1 on v0

v1 whole, which is shorter than its diff:
```python
import jax
import jax.numpy as jnp
from jax import lax
from jax.sharding import Mesh
from jax.sharding import PartitionSpec as P

EXPERT = ("y", "zh", "c")
DP = ("z", "x")
FAR = ("z", "y", "zh")
F32 = jnp.float32
BF16 = jnp.bfloat16


def exchange(tiles, axes):
    return lax.all_to_all(tiles, axes, split_axis=0, concat_axis=0, tiled=True)


def local(out_grad, gate_probs, expert_ids, saved_gate, saved_up, w_gate, w_up, w_down):
    nz, nx, ny, nh, nc = (lax.axis_size(a) for a in ("z", "x", "y", "zh", "c"))
    experts = ny * nh
    tokens, width = out_grad.shape
    slots = saved_gate.shape[1]
    cap = slots // (experts * nc)
    half = experts * cap
    hid = w_down.shape[1]
    chunk = cap * width
    padded = -(-chunk // 1024) * 1024

    iota = jnp.arange(experts, dtype=jnp.int32)
    chosen = (expert_ids[:, :, None] == iota[None, None, :]).astype(jnp.int32)
    per_token = jnp.sum(chosen, axis=1, dtype=jnp.int32)
    ranked = jnp.cumsum(per_token, axis=0, dtype=jnp.int32) - per_token
    position = jnp.sum(chosen * ranked[:, None, :], axis=2, dtype=jnp.int32)
    target = expert_ids * cap + position
    slot_iota = jnp.arange(half, dtype=jnp.int32)
    matches = slot_iota[:, None, None] == target[None, :, :]
    picker = jnp.any(matches, axis=2).astype(BF16)
    weighted = jnp.where(matches, gate_probs.astype(F32)[None, :, :], 0.0)
    weighted = jnp.sum(weighted, axis=2).astype(BF16)

    sent = jnp.dot(weighted, out_grad, preferred_element_type=F32).astype(BF16)
    sent = jnp.pad(sent.reshape(experts, chunk), ((0, 0), (0, padded - chunk)))
    sent = sent.reshape(experts, padded // 128, 128)
    sent = jnp.broadcast_to(sent[None], (nz, *sent.shape)).reshape(nz * experts, padded // 128, 128)
    got = exchange(sent, FAR).reshape(nz, experts, padded)
    mine = got[:, :, :chunk].reshape(nz, experts, cap, width)
    mine = mine.transpose(1, 2, 0, 3).reshape(half, nz * width)
    rows = lax.all_gather(mine, "x")
    rows = lax.all_gather(rows, "c")

    down = w_down[0].reshape(hid, nz, nx, width).transpose(2, 0, 1, 3).reshape(nx, hid, nz * width)
    gate_w = w_gate[0].reshape(nz, nx, width, hid).transpose(1, 0, 2, 3).reshape(nx, nz * width, hid)
    up_w = w_up[0].reshape(nz, nx, width, hid).transpose(1, 0, 2, 3).reshape(nx, nz * width, hid)

    def by_core(a):
        return a[0].reshape(experts, nc, cap, hid).transpose(1, 0, 2, 3).reshape(nc * half, hid)

    gate_pre = by_core(saved_gate).astype(F32)
    up_pre = by_core(saved_up).astype(F32)
    projected = sum(
        lax.dot_general(
            rows[:, k].reshape(nc * half, nz * width),
            down[k],
            (((1,), (1,)), ((), ())),
            preferred_element_type=F32,
        )
        for k in range(nx)
    )
    sig = jax.nn.sigmoid(gate_pre)
    gate_grad = (projected * up_pre * sig * (1.0 + gate_pre * (1.0 - sig))).astype(BF16)
    up_grad = (projected * gate_pre * sig).astype(BF16)
    both = jnp.concatenate([gate_grad, up_grad], axis=1)
    weights = jnp.concatenate([gate_w, up_w], axis=2)

    shares = jnp.stack(
        [
            lax.dot_general(both, weights[k], (((1,), (1,)), ((), ())), preferred_element_type=F32)
            .astype(BF16)
            .reshape(nc, half, nz * width)
            for k in range(nx)
        ],
        axis=1,
    )
    shares = jnp.sum(exchange(shares, "c").reshape(nc, nx, half, nz * width).astype(F32), axis=0)
    shares = jnp.sum(exchange(shares.astype(BF16), "x").astype(F32), axis=0).astype(BF16)
    back = shares.reshape(experts, cap, nz, width).transpose(2, 0, 1, 3)
    back = back.reshape(nz * experts, chunk)
    back = jnp.pad(back, ((0, 0), (0, padded - chunk)))
    back = exchange(back.reshape(nz * experts, padded // 128, 128), FAR)
    back = jnp.sum(back.reshape(nz, experts, padded).astype(F32), axis=0)
    back = back[:, :chunk].reshape(half, width).astype(BF16)
    return lax.dot_general(
        picker, back, (((0,), (0,)), ((), ())), preferred_element_type=F32
    ).astype(BF16)


def solution(mesh):
    split = Mesh(mesh.devices.reshape(16, 4, 4, 2, 2), ("z", "x", "y", "zh", "c"))
    return jax.shard_map(
        local,
        mesh=split,
        in_specs=(
            P(EXPERT, DP),
            P(EXPERT, None),
            P(EXPERT, None),
            P(EXPERT, None, DP),
            P(EXPERT, None, DP),
            P(EXPERT, None, DP),
            P(EXPERT, None, DP),
            P(EXPERT, DP, None),
        ),
        out_specs=P(EXPERT, DP),
        check_vma=False,
    )
```

time: 536 us -> 224 us (0.42)
  the two profiles are of different devices: /device:TPU:6 before, /device:TPU:32 now
where the time goes in v1:
time: 224 us; the launch traced here: 223 us
  blocking collectives  115 us (51%)
  waiting for transfers between devices  52 us (23%)
  starting transfers between devices  26.8 us (12%)
  between operations  13.7 us (6%)
  local copies, waits for them, and re-layouts  7.96 us (4%)
  other arithmetic  4.48 us (2%)
  matrix products  3.4 us (2%)
    all_to_all x3, blocking collectives, exchange(): return lax.all_to_all(tiles, axes, split_axis=0, concat_axis=0, tiled=True)  99.3 us
    all_to_all x1, waiting for transfers between devices, exchange(): return lax.all_to_all(tiles, axes, split_axis=0, concat_axis=0, tiled=True)  42 us
    all_to_all x1, starting transfers between devices, exchange(): return lax.all_to_all(tiles, axes, split_axis=0, concat_axis=0, tiled=True)  26.8 us
    all_gather x1, blocking collectives, local(): rows = lax.all_gather(mine, 'x')  15.8 us
    all_gather x1, waiting for transfers between devices, local(): rows = lax.all_gather(rows, 'c')  9.99 us
  transfers between devices with their start and end apart: 2, of which 2 were waited for; matrix products, arithmetic and copies ran while one was open for 0% of the time, Pallas kernels for 0%

profile of v1, /device:TPU:32, one launch (start us, length us, event | category | flops | bytes accessed | tf_op | source)
XLA Modules:
  0.0 223.4 jit_solution(7511832000838081441)
XLA Ops:
  6.5 0.7 convert_reduce_fusion
  7.2 0.1 copy.52
  7.3 0.1 reduce_window_sum.11
  7.4 0.1 copy.54
  7.5 0.7 select_reduce_fusion.1
  8.2 0.7 multiply_add_fusion
  8.9 0.7 convert_element_type.77
  9.5 0.1 select_reduce_fusion
  9.7 0.1 convolution_convert_fusion.4
  9.8 0.1 copy.55
  9.9 0.1 reshape.64
  10.1 75.2 %all_to_all.20 = bf16[128,8,128]{2,1,0:T(8,128)(2,1)S(1)} all-to-all(bf16[128,8,128]{2,1,0:T(8,128)(2,1)S(1)} %bitcast.89), channel_id=1, replica_groups=mesh['z'=16,'x'=4,'y'=4,'zh'=2,'c'=2] {'z','y','zh'}, dimensions={0} | all-to-all | bytes 524288 | tf_op jit(solution)/shard_map/all_to_all | solution.py:15
  85.3 0.1 reshape.66
  85.4 0.6 reshape.67
  86.1 0.4 copy.57
  86.5 0.6 all_gather_reshape.3
  87.2 15.8 %all_gather.9 = bf16[4,160,768]{2,1,0:T(8,128)(2,1)} all-gather(bf16[1,160,768]{2,1,0:T(8,128)(2,1)S(1)} %all_gather_reshape.3), channel_id=1, replica_groups=mesh['z'=16,'x'=4,'y'=4,'zh'=2,'c'=2] {'x'}, dimensions={0}, use_global_device_ids=true | all-gather | bytes 1228800 | tf_op jit(solution)/shard_map/all_gather | solution.py:48
  103.0 0.4 copy.58
  103.5 0.4 copy-done.5
  103.9 0.2 copy-done.2
  104.1 0.1 copy.61
  104.2 0.4 copy-done.3
  104.6 0.1 fusion.19
  104.7 10.0 %all-gather.3.cloned.1.call-done = bf16[8,160,768]{2,1,0:T(8,128)(2,1)} async-done(((bf16[4,160,768]{2,1,0:T(8,128)(2,1)}), bf16[8,160,768]{2,1,0:T(8,128)(2,1)}) %all-gather.3.cloned.1.call-update) | async-done | bytes 1966096 | tf_op jit(solution)/shard_map/all_gather | solution.py:49
  114.7 1.6 fusion.18
  116.3 0.3 fusion.20
  116.6 0.3 convolution_add_fusion.2
  116.9 0.3 convolution_add_fusion.1
  117.2 0.3 multiply_convert_fusion.1
  117.5 0.3 convolution_convert_fusion.3
  117.8 0.3 convolution_convert_fusion.2
  118.2 0.3 convolution_convert_fusion.1
  118.5 0.3 convolution_convert_fusion
  118.8 0.2 pad_maximum_fusion
  119.1 5.3 %all_to_all.21 = bf16[2,4,160,768]{3,2,1,0:T(8,128)(2,1)S(1)} all-to-all(bf16[2,4,160,768]{3,2,1,0:T(8,128)(2,1)S(1)} %pad_maximum_fusion), channel_id=1, replica_groups=mesh['z'=16,'x'=4,'y'=4,'zh'=2,'c'=2] {'c'}, dimensions={0} | all-to-all | bytes 3932160 | tf_op jit(solution)/shard_map/all_to_all | solution.py:15
  124.4 1.0 reduce_sum.63
  125.4 18.7 %all_to_all.22 = bf16[4,160,768]{2,1,0:T(8,128)(2,1)S(1)} all-to-all(bf16[4,160,768]{2,1,0:T(8,128)(2,1)S(1)} %reduce_sum.63), channel_id=1, replica_groups=mesh['z'=16,'x'=4,'y'=4,'zh'=2,'c'=2] {'x'}, dimensions={0} | all-to-all | bytes 1966080 | tf_op jit(solution)/shard_map/all_to_all | solution.py:15
  144.1 0.2 reduce_sum.64
  144.3 0.8 reshape.70
  145.1 0.2 copy.67
  145.3 0.5 reshape.71
  145.8 0.7 copy.68
  146.6 26.8 %all-to-all-start.3 = ((bf16[128,8,128]{2,1,0:T(8,128)(2,1)}), bf16[128,8,128]{2,1,0:T(8,128)(2,1)S(1)}, u32[]{:S(2)}, u32[]{:S(2)}) async-start(bf16[128,8,128]{2,1,0:T(8,128)(2,1)} %bitcast.44), calls=%async_computation.3 | async-start | bytes 524288 | tf_op jit(solution)/shard_map/all_to_all | solution.py:15
  173.4 0.1 fusion.12
  173.5 42.0 %all-to-all-done.3 = bf16[128,8,128]{2,1,0:T(8,128)(2,1)S(1)} async-done(((bf16[128,8,128]{2,1,0:T(8,128)(2,1)}), bf16[128,8,128]{2,1,0:T(8,128)(2,1)S(1)}, u32[]{:S(2)}, u32[]{:S(2)}) %all-to-all-start.3) | async-done | bytes 262176 | tf_op jit(solution)/shard_map/all_to_all | solution.py:15
  215.5 0.1 convert_element_type.94
  215.6 0.1 convert_element_type.96
  215.8 0.8 convolution_convert_fusion.5
  (24 shorter events, 0.3 us)
Async XLA Ops:
  6.5 3.1 %copy-start = (bf16[64,48]{0,1:T(8,128)(2,1)S(1)}, bf16[64,48]{0,1:T(8,128)(2,1)}, u32[]{:S(2)}) copy-start(bf16[64,48]{0,1:T(8,128)(2,1)} %param.8) | copy-start | bytes 18436
  6.5 108.1 %all-gather.3.cloned.1.call-start = ((), (), s32[]{:S(2)}) async-start(), calls=%async_computation.4 | async-start | bytes 2949120 | tf_op jit(solution)/shard_map/all_gather | solution.py:49
  86.0 16.9 %copy-start.1 = (bf16[1,128,3072]{2,1,0:T(8,128)(2,1)S(1)}, bf16[1,128,3072]{2,1,0:T(8,128)(2,1)}, u32[]{:S(2)}) copy-start(bf16[1,128,3072]{2,1,0:T(8,128)(2,1)} %param.15) | copy-start | bytes 2359300
  87.2 16.2 %copy-start.4 = (bf16[1,320,128]{2,1,0:T(8,128)(2,1)S(1)}, bf16[1,320,128]{2,1,0:T(8,128)(2,1)}, u32[]{:S(2)}) copy-start(bf16[1,320,128]{2,1,0:T(8,128)(2,1)} %param.12) | copy-start | bytes 245764
  102.9 0.9 copy-start.5
  103.0 1.1 copy-start.2
  103.4 1.2 copy-start.3
  146.6 68.9 %all-to-all-start.3 = ((bf16[128,8,128]{2,1,0:T(8,128)(2,1)}), bf16[128,8,128]{2,1,0:T(8,128)(2,1)S(1)}, u32[]{:S(2)}, u32[]{:S(2)}) async-start(bf16[128,8,128]{2,1,0:T(8,128)(2,1)} %bitcast.44), calls=%async_computation.3 | async-start | bytes 524288 | tf_op jit(solution)/shard_map/all_to_all | solution.py:15
Sparse Core Ops, SparseCore 0:
  103.1 11.5 all-gather.2

commit v2 on v1

v2 whole, which is shorter than its diff:
```python
import jax
import jax.numpy as jnp
from jax import lax
from jax.sharding import Mesh
from jax.sharding import PartitionSpec as P

EXPERT = ("y", "zh", "c")
DP = ("za", "zb", "x")
FAR = ("za", "y", "zh")
F32 = jnp.float32
BF16 = jnp.bfloat16


def exchange(tiles, axes):
    return lax.all_to_all(tiles, axes, split_axis=0, concat_axis=0, tiled=True)


def swap(value):
    return lax.ppermute(value, "c", [(0, 1), (1, 0)])


def times_t(a, b):
    return lax.dot_general(a, b, (((1,), (1,)), ((), ())), preferred_element_type=F32)


def local(out_grad, gate_probs, expert_ids, saved_gate, saved_up, w_gate, w_up, w_down):
    na, nb, nx, ny, nh, nc = (lax.axis_size(a) for a in ("za", "zb", "x", "y", "zh", "c"))
    experts = ny * nh
    width = out_grad.shape[1]
    slots = saved_gate.shape[1]
    cap = slots // (experts * nc)
    half = experts * cap
    hid = w_down.shape[1]
    span = na * nb * width
    chunk = cap * width
    padded = -(-chunk // 1024) * 1024
    tile = (padded // 128, 128)
    first_core = lax.axis_index("c") == 0

    iota = jnp.arange(experts, dtype=jnp.int32)
    chosen = (expert_ids[:, :, None] == iota[None, None, :]).astype(jnp.int32)
    per_token = jnp.sum(chosen, axis=1, dtype=jnp.int32)
    ranked = jnp.cumsum(per_token, axis=0, dtype=jnp.int32) - per_token
    position = jnp.sum(chosen * ranked[:, None, :], axis=2, dtype=jnp.int32)
    target = expert_ids * cap + position
    slot_iota = jnp.arange(half, dtype=jnp.int32)
    matches = slot_iota[:, None, None] == target[None, :, :]
    picker = jnp.any(matches, axis=2).astype(BF16)
    weighted = jnp.where(matches, gate_probs.astype(F32)[None, :, :], 0.0)
    weighted = jnp.sum(weighted, axis=2).astype(BF16)

    sent = jnp.dot(weighted, out_grad, preferred_element_type=F32).astype(BF16)
    sent = jnp.pad(sent.reshape(experts, chunk), ((0, 0), (0, padded - chunk)))
    sent = sent.reshape(experts, *tile)
    sent = jnp.broadcast_to(sent[None], (na, *sent.shape)).reshape(na * experts, *tile)
    got = exchange(sent, FAR)
    got = jnp.broadcast_to(got[None], (nb, *got.shape)).reshape(nb * na * experts, *tile)
    got = exchange(got.reshape(nb, na * experts * tile[0], 128), "zb")
    got = got.reshape(nb, na, experts, padded)[..., :chunk]
    got = got.reshape(nb, na, experts, cap, width).transpose(2, 3, 1, 0, 4)
    own_rows = lax.all_gather(got.reshape(half, span), "x")
    other_rows = swap(own_rows)

    down = w_down[0].reshape(hid, na * nb, nx, width).transpose(2, 0, 1, 3).reshape(nx, hid, span)
    gate_w = w_gate[0].reshape(na * nb, nx, width, hid).transpose(1, 0, 2, 3).reshape(nx, span, hid)
    up_w = w_up[0].reshape(na * nb, nx, width, hid).transpose(1, 0, 2, 3).reshape(nx, span, hid)

    def by_core(a):
        parts = a[0].reshape(experts, nc, cap, hid).transpose(1, 0, 2, 3).reshape(nc, half, hid)
        return (
            jnp.where(first_core, parts[0], parts[1]).astype(F32),
            jnp.where(first_core, parts[1], parts[0]).astype(F32),
        )

    gates = by_core(saved_gate)
    ups = by_core(saved_up)

    def through(rows, gate_pre, up_pre):
        projected = sum(times_t(rows[k], down[k]) for k in range(nx))
        sig = jax.nn.sigmoid(gate_pre)
        gate_grad = (projected * up_pre * sig * (1.0 + gate_pre * (1.0 - sig))).astype(BF16)
        up_grad = (projected * gate_pre * sig).astype(BF16)
        return jnp.stack(
            [
                (times_t(gate_grad, gate_w[k]) + times_t(up_grad, up_w[k])).astype(BF16)
                for k in range(nx)
            ]
        )

    for_other = through(other_rows, gates[1], ups[1])
    for_own = through(own_rows, gates[0], ups[0])
    shares = (for_own.astype(F32) + swap(for_other).astype(F32)).astype(BF16)
    shares = jnp.sum(exchange(shares, "x").astype(F32), axis=0).astype(BF16)
    back = shares.reshape(experts, cap, na, nb, width).transpose(3, 2, 0, 1, 4)
    back = back.reshape(nb, na * experts, chunk)
    back = jnp.pad(back, ((0, 0), (0, 0), (0, padded - chunk)))
    back = exchange(back.reshape(nb, na * experts * tile[0], 128), "zb")
    back = jnp.sum(back.astype(F32), axis=0).astype(BF16)
    back = exchange(back.reshape(na * experts, *tile), FAR)
    back = jnp.sum(back.reshape(na, experts, padded).astype(F32), axis=0)
    back = back[:, :chunk].reshape(half, width).astype(BF16)
    return lax.dot_general(
        picker, back, (((0,), (0,)), ((), ())), preferred_element_type=F32
    ).astype(BF16)


def solution(mesh):
    split = Mesh(mesh.devices.reshape(4, 4, 4, 4, 2, 2), ("za", "zb", "x", "y", "zh", "c"))
    return jax.shard_map(
        local,
        mesh=split,
        in_specs=(
            P(EXPERT, DP),
            P(EXPERT, None),
            P(EXPERT, None),
            P(EXPERT, None, DP),
            P(EXPERT, None, DP),
            P(EXPERT, None, DP),
            P(EXPERT, None, DP),
            P(EXPERT, DP, None),
        ),
        out_specs=P(EXPERT, DP),
        check_vma=False,
    )
```

time: 224 us -> 163 us (0.73)
  waiting for transfers between devices: 52 us -> 28.7 us
  blocking collectives: 115 us -> 99.1 us
  between operations: 13.7 us -> 0.49 us
  starting transfers between devices: 26.8 us -> 14.3 us
  matrix products: 3.4 us -> 6.24 us
    all_to_all x1 -> x2, starting transfers between devices: 26.8 us -> 10.2 us  [exchange(): return lax.all_to_all(tiles, axes, split_axis=0, concat_axis=0, tiled=True)]
    all_to_all x1 -> x2, waiting for transfers between devices: 42 us -> 26.6 us  [exchange(): return lax.all_to_all(tiles, axes, split_axis=0, concat_axis=0, tiled=True)]
    all_to_all x3, blocking collectives: 99.3 us -> 84.1 us  [exchange(): return lax.all_to_all(tiles, axes, split_axis=0, concat_axis=0, tiled=True)]
    all_gather x1 -> x0, waiting for transfers between devices: 9.99 us -> none  [local(): rows = lax.all_gather(rows, 'c')]
    ppermute x0 -> x2, starting transfers between devices: none -> 4.1 us  [swap(): return lax.ppermute(value, 'c', [(0, 1), (1, 0)])]
    dot_general x8 -> x24, matrix products: 2.48 us -> 5.32 us  [times_t(): lax.dot_general(a, b, (((1,), (1,)), ((), ())), preferred_element_type=F32)]
  transfers between devices with their start and end apart: 2 -> 4, of which waited for: 2 -> 4; matrix products, arithmetic and copies ran while one was open for 0% -> 4% of each run, Pallas kernels for 0% -> 0%
where the time goes in v2:
time: 163 us
  blocking collectives  99.1 us (61%)
  waiting for transfers between devices  28.7 us (18%)
  starting transfers between devices  14.3 us (9%)
  local copies, waits for them, and re-layouts  9.56 us (6%)
  matrix products  6.24 us (4%)
  other arithmetic  4.32 us (3%)
    all_to_all x3, blocking collectives, exchange(): return lax.all_to_all(tiles, axes, split_axis=0, concat_axis=0, tiled=True)  84.1 us
    all_to_all x2, waiting for transfers between devices, exchange(): return lax.all_to_all(tiles, axes, split_axis=0, concat_axis=0, tiled=True)  26.6 us
    all_gather x1, blocking collectives, local(): own_rows = lax.all_gather(got.reshape(half, span), 'x')  15 us
    all_to_all x2, starting transfers between devices, exchange(): return lax.all_to_all(tiles, axes, split_axis=0, concat_axis=0, tiled=True)  10.2 us
    dot_general x24, matrix products, times_t(): lax.dot_general(a, b, (((1,), (1,)), ((), ())), preferred_element_type=F32)  5.32 us
    ppermute x2, starting transfers between devices, swap(): return lax.ppermute(value, 'c', [(0, 1), (1, 0)])  4.1 us
  transfers between devices with their start and end apart: 4, of which 4 were waited for; matrix products, arithmetic and copies ran while one was open for 4% of the time, Pallas kernels for 0%

profile of v2, /device:TPU:32, one launch (start us, length us, event | category | flops | bytes accessed | tf_op | source)
XLA Modules:
  0.0 162.8 jit_solution(290091754412109569)
XLA Ops:
  0.0 0.8 convert_reduce_fusion
  1.0 0.7 select_reduce_fusion.1
  1.7 0.7 multiply_add_fusion
  2.4 0.7 convert_element_type.104
  3.6 56.3 %all_to_all.25 = bf16[32,8,128]{2,1,0:T(8,128)(2,1)S(1)} all-to-all(bf16[32,8,128]{2,1,0:T(8,128)(2,1)S(1)} %bitcast.163), channel_id=1, replica_groups=mesh['za'=4,'zb'=4,'x'=4,'y'=4,'zh'=2,'c'=2] {'za','y','zh'}, dimensions={0} | all-to-all | bytes 131072 | tf_op jit(solution)/shard_map/all_to_all | solution.py:15
  59.9 0.7 broadcast_in_dim.38
  60.7 4.7 %all-to-all-start.1 = ((bf16[4,256,128]{2,1,0:T(8,128)(2,1)}), bf16[4,256,128]{2,1,0:T(8,128)(2,1)S(1)}, u32[]{:S(2)}, u32[]{:S(2)}) async-start(bf16[4,256,128]{2,1,0:T(8,128)(2,1)} %broadcast_in_dim.38), calls=%async_computation.1 | async-start | bytes 524288 | tf_op jit(solution)/shard_map/all_to_all | solution.py:15
  65.3 0.4 copy.44
  65.7 0.5 copy-done.7
  66.3 0.6 reshape.109
  66.9 0.6 reshape.106
  67.6 0.6 reshape.107
  68.2 0.8 fusion.26
  69.0 1.1 copy-done.3
  70.2 1.4 all-to-all-done.1
  71.6 0.6 reshape.101
  72.3 0.5 copy.43
  72.8 0.7 all_gather_reshape.3
  73.5 15.0 %all_gather.3 = bf16[4,160,768]{2,1,0:T(8,128)(2,1)S(1)} all-gather(bf16[1,160,768]{2,1,0:T(8,128)(2,1)S(1)} %all_gather_reshape.3), channel_id=1, replica_groups=mesh['za'=4,'zb'=4,'x'=4,'y'=4,'zh'=2,'c'=2] {'x'}, dimensions={0}, use_global_device_ids=true | all-gather | bytes 1228800 | tf_op jit(solution)/shard_map/all_gather | solution.py:61
  88.4 2.0 %collective-permute-start = (bf16[4,160,768]{2,1,0:T(8,128)(2,1)S(1)}, bf16[4,160,768]{2,1,0:T(8,128)(2,1)S(1)}, u32[]{:S(2)}, u32[]{:S(2)}) collective-permute-start(bf16[4,160,768]{2,1,0:T(8,128)(2,1)S(1)} %all_gather.3), channel_id=1, source_target_pairs={{0,1},{1,0},{2,3},{3,2},{4,5},{5,4},{6,7},{7,6},{8,9},{9,8},{10,11... | collective-permute-start | bytes 2949128 | tf_op jit(solution)/shard_map/ppermute | solution.py:19
  91.2 0.2 multiply_convert_fusion.2
  91.9 1.1 collective-permute-done
  93.7 0.2 multiply_convert_fusion
  93.9 0.2 fusion.31
  94.2 0.2 fusion.32
  94.4 0.2 fusion.33
  94.6 0.2 fusion.34
  94.9 0.2 fusion.11
  95.1 0.2 fusion.10
  95.3 0.2 fusion.9
  95.6 0.2 fusion.8
  95.9 2.0 %collective-permute-start.1 = (bf16[4,160,768]{2,1,0:T(8,128)(2,1)S(1)}, bf16[4,160,768]{2,1,0:T(8,128)(2,1)S(1)}, u32[]{:S(2)}, u32[]{:S(2)}) collective-permute-start(bf16[4,160,768]{2,1,0:T(8,128)(2,1)S(1)} %pad_maximum_fusion), channel_id=1, source_target_pairs={{0,1},{1,0},{2,3},{3,2},{4,5},{5,4},{6,7},{7,6},{8,9},{9,8},{10,11... | collective-permute-start | bytes 2949128 | tf_op jit(solution)/shard_map/ppermute | solution.py:19
  98.0 0.2 fusion.15
  98.2 0.2 fusion.14
  98.5 0.2 fusion.29
  98.7 0.2 fusion.13
  98.9 0.2 fusion.30
  99.1 0.2 fusion.12
  99.4 1.0 collective-permute-done.1
  100.4 0.2 add_convert_fusion
  100.6 18.0 %all_to_all.26 = bf16[4,160,768]{2,1,0:T(8,128)(2,1)S(1)} all-to-all(bf16[4,160,768]{2,1,0:T(8,128)(2,1)S(1)} %add_convert_fusion), channel_id=1, replica_groups=mesh['za'=4,'zb'=4,'x'=4,'y'=4,'zh'=2,'c'=2] {'x'}, dimensions={0} | all-to-all | bytes 1966080 | tf_op jit(solution)/shard_map/all_to_all | solution.py:15
  118.8 0.8 reshape.102
  119.8 0.5 reshape.103
  120.4 9.8 %all_to_all.27 = bf16[4,256,128]{2,1,0:T(8,128)(2,1)S(1)} all-to-all(bf16[4,256,128]{2,1,0:T(8,128)(2,1)S(1)} %reshape.104), channel_id=1, replica_groups=mesh['za'=4,'zb'=4,'x'=4,'y'=4,'zh'=2,'c'=2] {'zb'}, dimensions={0} | all-to-all | bytes 524288 | tf_op jit(solution)/shard_map/all_to_all | solution.py:15
  130.2 0.7 reduce_sum.64
  130.9 5.6 %all-to-all-start.4 = ((bf16[32,8,128]{2,1,0:T(8,128)(2,1)}), bf16[32,8,128]{2,1,0:T(8,128)(2,1)S(1)}, u32[]{:S(2)}, u32[]{:S(2)}) async-start(bf16[32,8,128]{2,1,0:T(8,128)(2,1)} %bitcast.44), calls=%async_computation.4 | async-start | bytes 131072 | tf_op jit(solution)/shard_map/all_to_all | solution.py:15
  136.6 25.2 %all-to-all-done.4 = bf16[32,8,128]{2,1,0:T(8,128)(2,1)S(1)} async-done(((bf16[32,8,128]{2,1,0:T(8,128)(2,1)}), bf16[32,8,128]{2,1,0:T(8,128)(2,1)S(1)}, u32[]{:S(2)}, u32[]{:S(2)}) %all-to-all-start.4) | async-done | bytes 65568 | tf_op jit(solution)/shard_map/all_to_all | solution.py:15
  162.0 0.8 convolution_convert_fusion.1
  (55 shorter events, 3.6 us)
Async XLA Ops:
  0.0 3.2 %copy-start = (bf16[64,48]{0,1:T(8,128)(2,1)S(1)}, bf16[64,48]{0,1:T(8,128)(2,1)}, u32[]{:S(2)}) copy-start(bf16[64,48]{0,1:T(8,128)(2,1)} %param.8) | copy-start | bytes 18436
  0.0 65.3 %copy-start.1 = (bf16[1,128,3072]{2,1,0:T(8,128)(2,1)S(1)}, bf16[1,128,3072]{2,1,0:T(8,128)(2,1)}, u32[]{:S(2)}) copy-start(bf16[1,128,3072]{2,1,0:T(8,128)(2,1)} %param.15) | copy-start | bytes 2359300
  60.7 5.0 %copy-start.6 = (bf16[1,320,128]{2,1,0:T(8,128)(2,1)S(1)}, bf16[1,320,128]{2,1,0:T(8,128)(2,1)}, u32[]{:S(2)}) copy-start(bf16[1,320,128]{2,1,0:T(8,128)(2,1)} %param.12) | copy-start | bytes 245764
  60.7 10.9 %all-to-all-start.1 = ((bf16[4,256,128]{2,1,0:T(8,128)(2,1)}), bf16[4,256,128]{2,1,0:T(8,128)(2,1)S(1)}, u32[]{:S(2)}, u32[]{:S(2)}) async-start(bf16[4,256,128]{2,1,0:T(8,128)(2,1)} %broadcast_in_dim.38), calls=%async_computation.1 | async-start | bytes 524288 | tf_op jit(solution)/shard_map/all_to_all | solution.py:15
  65.3 0.9 copy-start.7
  66.9 2.1 %copy-start.2 = (bf16[1,3072,128]{2,1,0:T(8,128)(2,1)S(1)}, bf16[1,3072,128]{2,1,0:T(8,128)(2,1)}, u32[]{:S(2)}) copy-start(bf16[1,3072,128]{2,1,0:T(8,128)(2,1)} %param.13) | copy-start | bytes 2359300
  69.0 1.1 copy-start.3
  72.8 17.7 %copy-start.4 = (bf16[1,128,16,48]{1,3,0,2:T(8,128)(2,1)S(1)}, bf16[1,128,16,48]{1,3,0,2:T(8,128)(2,1)}, u32[]{:S(2)}) copy-start(bf16[1,128,16,48]{1,3,0,2:T(8,128)(2,1)} %get-tuple-element.13) | copy-start | bytes 589828
  88.4 2.7 %copy-start.5 = (bf16[1,128,16,48]{1,3,0,2:T(8,128)(2,1)S(1)}, bf16[1,128,16,48]{1,3,0,2:T(8,128)(2,1)}, u32[]{:S(2)}) copy-start(bf16[1,128,16,48]{1,3,0,2:T(8,128)(2,1)} %get-tuple-element.14) | copy-start | bytes 589828
  88.4 2.7 %copy-start.9 = (f32[160,128]{1,0:T(8,128)S(1)}, f32[160,128]{1,0:T(8,128)}, u32[]{:S(2)}) copy-start(f32[160,128]{1,0:T(8,128)} %reshape.106) | copy-start | bytes 245764
  88.4 2.7 %copy-start.10 = (f32[160,128]{1,0:T(8,128)S(1)}, f32[160,128]{1,0:T(8,128)}, u32[]{:S(2)}) copy-start(f32[160,128]{1,0:T(8,128)} %reshape.107) | copy-start | bytes 245764
  88.4 4.6 %collective-permute-start = (bf16[4,160,768]{2,1,0:T(8,128)(2,1)S(1)}, bf16[4,160,768]{2,1,0:T(8,128)(2,1)S(1)}, u32[]{:S(2)}, u32[]{:S(2)}) collective-permute-start(bf16[4,160,768]{2,1,0:T(8,128)(2,1)S(1)} %all_gather.3), channel_id=1, source_target_pairs={{0,1},{1,0},{2,3},{3,2},{4,5},{5,4},{6,7},{7,6},{8,9},{9,8},{10,11... | collective-permute-start | bytes 2949128 | tf_op jit(solution)/shard_map/ppermute | solution.py:19
  91.6 2.0 %copy-start.8 = (f32[160,128]{1,0:T(8,128)S(1)}, f32[160,128]{1,0:T(8,128)}, u32[]{:S(2)}) copy-start(f32[160,128]{1,0:T(8,128)} %reshape.109) | copy-start | bytes 245764
  95.9 4.5 %collective-permute-start.1 = (bf16[4,160,768]{2,1,0:T(8,128)(2,1)S(1)}, bf16[4,160,768]{2,1,0:T(8,128)(2,1)S(1)}, u32[]{:S(2)}, u32[]{:S(2)}) collective-permute-start(bf16[4,160,768]{2,1,0:T(8,128)(2,1)S(1)} %pad_maximum_fusion), channel_id=1, source_target_pairs={{0,1},{1,0},{2,3},{3,2},{4,5},{5,4},{6,7},{7,6},{8,9},{9,8},{10,11... | collective-permute-start | bytes 2949128 | tf_op jit(solution)/shard_map/ppermute | solution.py:19
  130.9 30.9 %all-to-all-start.4 = ((bf16[32,8,128]{2,1,0:T(8,128)(2,1)}), bf16[32,8,128]{2,1,0:T(8,128)(2,1)S(1)}, u32[]{:S(2)}, u32[]{:S(2)}) async-start(bf16[32,8,128]{2,1,0:T(8,128)(2,1)} %bitcast.44), calls=%async_computation.4 | async-start | bytes 131072 | tf_op jit(solution)/shard_map/all_to_all | solution.py:15

commit v3 on v2

v3 whole, which is shorter than its diff:
```python
import functools

import jax
import jax.numpy as jnp
from jax import lax
from jax.experimental import pallas as pl
from jax.experimental.pallas import tpu as pltpu
from jax.sharding import Mesh
from jax.sharding import PartitionSpec as P

EXPERT = ("y", "zh", "c")
DP = ("za", "zb", "x")
FAR = ("za", "y", "zh")
F32 = jnp.float32
BF16 = jnp.bfloat16


def exchange(tiles, axes):
    return lax.all_to_all(tiles, axes, split_axis=0, concat_axis=0, tiled=True)


def swap(value):
    return lax.ppermute(value, "c", [(0, 1), (1, 0)])


def times_t(a, b):
    return lax.dot_general(a, b, (((1,), (1,)), ((), ())), preferred_element_type=F32)


PARTS = 4


def counted(shape, dim):
    return lax.broadcasted_iota(jnp.int32, shape, dim)


def placing(part, width):
    feature, lane = counted((width, 128), 0), counted((width, 128), 1)
    if part < 2:
        hit = lane == feature + part * width
    elif part == 2:
        hit = (lane == feature + 2 * width) & (feature < width // 2)
    else:
        hit = (lane == feature + 2 * width - width // 2) & (feature >= width // 2)
    return hit.astype(F32).astype(BF16)


def dispatch_kernel(ids_ref, prob_ref, grad_ref, tile_ref, pick_ref):
    copies, rows, _ = tile_ref.shape
    width, tokens = grad_ref.shape
    expert = counted((rows, tokens), 0) >> 3
    row = counted((rows, tokens), 0) & 7
    first = ids_ref[0:1, :] == expert
    second = ids_ref[1:2, :] == expert
    named = first | second
    prob = prob_ref[...].astype(F32)
    weight = jnp.where(first, prob[0:1, :], 0.0) + jnp.where(second, prob[1:2, :], 0.0)
    earlier = counted((tokens, tokens), 0) < counted((tokens, tokens), 1)
    slot = jnp.dot(
        named.astype(F32).astype(BF16),
        earlier.astype(F32).astype(BF16),
        preferred_element_type=F32,
    ).astype(jnp.int32)
    grad = grad_ref[...]
    total = jnp.zeros((rows, 128), F32)
    for part in range(PARTS):
        hit = named & (slot == row + (0, 8, 16, 12)[part])
        if part == 2:
            hit = hit & (row < 4)
        if part == 3:
            hit = hit & (row >= 4)
        pick_ref[part] = hit.astype(F32).astype(BF16)
        mine = times_t(jnp.where(hit, weight, 0.0).astype(BF16), grad).astype(BF16)
        total = total + jnp.dot(mine, placing(part, width), preferred_element_type=F32)
    tile = total.astype(BF16)
    for k in range(copies):
        tile_ref[k] = tile


def unpack_kernel(width, got_ref, out_ref):
    nb, na, rows, _ = got_ref.shape
    short = rows // 2
    at, source = counted((rows, rows), 0), counted((rows, rows), 1)
    number = at & (short - 1)
    wanted = (number >> 2) * 8 + (number & 3) + jnp.where(at >= short, 4, 0)
    halves = (source == wanted).astype(F32).astype(BF16)
    whole, upper, lower = [], [], []
    for a in range(na):
        for b in range(nb):
            tile = got_ref[b, a]
            whole.append(tile[:, :width])
            upper.append(tile[:, width : 2 * width])
            rest = jnp.dot(halves, tile, preferred_element_type=F32).astype(BF16)
            lower.append(rest[:short, 2 * width : 2 * width + width // 2])
            lower.append(rest[short:, 2 * width : 2 * width + width // 2])
    out_ref[:rows, :] = jnp.concatenate(whole, axis=1)
    out_ref[rows : 2 * rows, :] = jnp.concatenate(upper, axis=1)
    out_ref[2 * rows :, :] = jnp.concatenate(lower, axis=1)


def pack_kernel(width, in_ref, out_ref):
    nb, na, rows, _ = out_ref.shape
    peers = in_ref.shape[0]
    short = rows // 2
    total = in_ref[0].astype(F32)
    for k in range(1, peers):
        total = total + in_ref[k].astype(F32)
    total = total.astype(BF16)
    at, source = counted((rows, short), 0), counted((rows, short), 1)
    wanted = (at >> 3) * 4 + (at & 3)
    low = ((source == wanted) & ((at & 7) < 4)).astype(F32).astype(BF16)
    high = ((source == wanted) & ((at & 7) >= 4)).astype(F32).astype(BF16)
    lows = jnp.dot(low, total[2 * rows :], preferred_element_type=F32).astype(BF16)
    highs = jnp.dot(high, total[2 * rows :], preferred_element_type=F32).astype(BF16)
    blank = jnp.zeros((rows, 128 - 2 * width - width // 2), BF16)
    for a in range(na):
        for b in range(nb):
            at = (a * nb + b) * width
            half = lows[:, at : at + width // 2] + highs[:, at + width // 2 : at + width]
            out_ref[b, a] = jnp.concatenate(
                [total[:rows, at : at + width], total[rows : 2 * rows, at : at + width], half, blank],
                axis=1,
            )


def final_kernel(got_ref, pick_ref, out_ref):
    width = out_ref.shape[0]
    total = got_ref[0].astype(F32)
    for k in range(1, got_ref.shape[0]):
        total = total + got_ref[k].astype(F32)
    total = total.astype(BF16)
    out = jnp.zeros(out_ref.shape, F32)
    for part in range(PARTS):
        rows = times_t(placing(part, width), total).astype(BF16)
        out = out + jnp.dot(rows, pick_ref[part], preferred_element_type=F32)
    out_ref[...] = out.astype(BF16)


def call(kernel, name, out, *args):
    shapes = [jax.ShapeDtypeStruct(s, BF16) for s in out]
    whole = pl.BlockSpec(memory_space=pltpu.VMEM)
    return pl.pallas_call(
        kernel,
        name=name,
        out_shape=shapes,
        in_specs=[whole] * len(args),
        out_specs=[whole] * len(out),
        cost_estimate=pl.CostEstimate(flops=4000000, bytes_accessed=300000, transcendentals=0),
    )(*args)


def local(out_grad, gate_probs, expert_ids, saved_gate, saved_up, w_gate, w_up, w_down):
    na, nb, nx, ny, nh, nc = (lax.axis_size(a) for a in ("za", "zb", "x", "y", "zh", "c"))
    experts = ny * nh
    tokens, width = out_grad.shape
    slots = saved_gate.shape[1]
    cap = slots // (experts * nc)
    half = experts * cap
    hid = w_down.shape[1]
    span = na * nb * width
    rows = experts * 8
    assert cap == 20 and 2 * width + width // 2 <= 128
    first_core = lax.axis_index("c") == 0

    sent, picks = call(
        dispatch_kernel,
        "dispatch",
        [(na, rows, 128), (PARTS, rows, tokens)],
        expert_ids.T,
        gate_probs.T,
        out_grad.T,
    )
    got = exchange(sent.reshape(na * experts, 8, 128), FAR)
    got = jnp.broadcast_to(got.reshape(1, na * rows, 128), (nb, na * rows, 128))
    got = exchange(got, "zb").reshape(nb, na, rows, 128)
    (got,) = call(functools.partial(unpack_kernel, width), "unpack", [(half, span)], got)
    own_rows = lax.all_gather(got, "x")
    other_rows = swap(own_rows)

    down = w_down[0].reshape(hid, na * nb, nx, width).transpose(2, 0, 1, 3).reshape(nx, hid, span)
    gate_w = w_gate[0].reshape(na * nb, nx, width, hid).transpose(1, 0, 2, 3).reshape(nx, span, hid)
    up_w = w_up[0].reshape(na * nb, nx, width, hid).transpose(1, 0, 2, 3).reshape(nx, span, hid)

    def by_core(a):
        parts = a[0].reshape(experts, nc, cap, hid)
        parts = jnp.stack(
            [
                jnp.concatenate(
                    [parts[:, k, at:to].reshape(-1, hid) for at, to in ((0, 8), (8, 16), (16, cap))]
                )
                for k in range(nc)
            ]
        )
        return (
            jnp.where(first_core, parts[0], parts[1]).astype(F32),
            jnp.where(first_core, parts[1], parts[0]).astype(F32),
        )

    gates = by_core(saved_gate)
    ups = by_core(saved_up)

    def through(rows, gate_pre, up_pre):
        projected = sum(times_t(rows[k], down[k]) for k in range(nx))
        sig = jax.nn.sigmoid(gate_pre)
        gate_grad = (projected * up_pre * sig * (1.0 + gate_pre * (1.0 - sig))).astype(BF16)
        up_grad = (projected * gate_pre * sig).astype(BF16)
        return jnp.stack(
            [
                (times_t(gate_grad, gate_w[k]) + times_t(up_grad, up_w[k])).astype(BF16)
                for k in range(nx)
            ]
        )

    for_other = through(other_rows, gates[1], ups[1])
    for_own = through(own_rows, gates[0], ups[0])
    shares = (for_own.astype(F32) + swap(for_other).astype(F32)).astype(BF16)
    shares = exchange(shares, "x")
    (back,) = call(functools.partial(pack_kernel, width), "pack", [(nb, na, rows, 128)], shares)
    back = exchange(back.reshape(nb, na * rows, 128), "zb")
    back = jnp.sum(back.astype(F32), axis=0).astype(BF16)
    back = exchange(back.reshape(na * experts, 8, 128), FAR).reshape(na, rows, 128)
    (out,) = call(final_kernel, "pick", [(width, tokens)], back, picks)
    return out.T


def solution(mesh):
    split = Mesh(mesh.devices.reshape(4, 4, 4, 4, 2, 2), ("za", "zb", "x", "y", "zh", "c"))
    return jax.shard_map(
        local,
        mesh=split,
        in_specs=(
            P(EXPERT, DP),
            P(EXPERT, None),
            P(EXPERT, None),
            P(EXPERT, None, DP),
            P(EXPERT, None, DP),
            P(EXPERT, None, DP),
            P(EXPERT, None, DP),
            P(EXPERT, DP, None),
        ),
        out_specs=P(EXPERT, DP),
        check_vma=False,
    )
```

time: 163 us -> 169 us (1.037)
  blocking collectives: 99.1 us -> 131 us
  waiting for transfers between devices: 28.7 us -> 6.22 us
  Pallas kernels: 0 us -> 7.9 us
  starting transfers between devices: 14.3 us -> 8.61 us
  local copies, waits for them, and re-layouts: 9.56 us -> 4.34 us
  other arithmetic: 4.32 us -> 0.48 us
  matrix products: 6.24 us -> 9.06 us
    all_to_all x3 -> x4, blocking collectives: 84.1 us -> 116 us  [exchange(): return lax.all_to_all(tiles, axes, split_axis=0, concat_axis=0, tiled=True)]
    all_to_all x2 -> x1, waiting for transfers between devices: 26.6 us -> 3.93 us  [exchange(): return lax.all_to_all(tiles, axes, split_axis=0, concat_axis=0, tiled=True)]
    pallas_call x0 -> x4, Pallas kernels: none -> 7.9 us  [call(): pl.pallas_call(kernel, name=name, out_shape=shapes, in_specs=[whole] * le...]
    all_to_all x2 -> x1, starting transfers between devices: 10.2 us -> 4.64 us  [exchange(): return lax.all_to_all(tiles, axes, split_axis=0, concat_axis=0, tiled=True)]
    dot_general x24, matrix products: 5.32 us -> 9.06 us  [times_t(): lax.dot_general(a, b, (((1,), (1,)), ((), ())), preferred_element_type=F32)]
    reshape x6 -> x0, local copies, waits for them, and re-layouts: 2.24 us -> none  [the longest x1 0.79 us: local(): back = shares.reshape(experts, cap, na, nb, width).transpose(3, 2, 0, 1, 4)]
    convert_element_type x7 -> x0, local copies, waits for them, and re-layouts: 2.16 us -> none  [the longest x2 1.27 us: by_core(): jnp.where(first_core, parts[0], parts[1]).astype(F32)]
    reduce_sum x5 -> x0, other arithmetic: 1.74 us -> none  [the longest x1 0.76 us: local(): per_token = jnp.sum(chosen, axis=1, dtype=jnp.int32)]
  transfers between devices with their start and end apart: 4 -> 3, of which waited for: 4 -> 3; matrix products, arithmetic and copies ran while one was open for 4% -> 3% of each run, Pallas kernels for 0% -> 0%
where the time goes in v3:
time: 169 us; the launch traced here: 168 us
  blocking collectives  131 us (78%)
  matrix products  9.06 us (5%)
  starting transfers between devices  8.61 us (5%)
  Pallas kernels  7.9 us (5%)
  waiting for transfers between devices  6.22 us (4%)
  local copies, waits for them, and re-layouts  4.34 us (3%)
    all_to_all x4, blocking collectives, exchange(): return lax.all_to_all(tiles, axes, split_axis=0, concat_axis=0, tiled=True)  116 us
    all_gather x1, blocking collectives, local(): own_rows = lax.all_gather(got, 'x')  15.2 us
    dot_general x24, matrix products, times_t(): lax.dot_general(a, b, (((1,), (1,)), ((), ())), preferred_element_type=F32)  9.06 us
    pallas_call x4, Pallas kernels, call(): pl.pallas_call(kernel, name=name, out_shape=shapes, in_specs=[whole] * le...  7.9 us
    all_to_all x1, starting transfers between devices, exchange(): return lax.all_to_all(tiles, axes, split_axis=0, concat_axis=0, tiled=True)  4.64 us
    ppermute x2, starting transfers between devices, swap(): return lax.ppermute(value, 'c', [(0, 1), (1, 0)])  3.97 us
    all_to_all x1, waiting for transfers between devices, exchange(): return lax.all_to_all(tiles, axes, split_axis=0, concat_axis=0, tiled=True)  3.93 us
  transfers between devices with their start and end apart: 3, of which 3 were waited for; matrix products, arithmetic and copies ran while one was open for 3% of the time, Pallas kernels for 0%

profile of v3, /device:TPU:32, one launch (start us, length us, event | category | flops | bytes accessed | tf_op | source)
XLA Modules:
  0.0 168.4 jit_solution(7935404320467876935)
XLA Ops:
  0.0 1.9 %dispatch.1 = (bf16[4,64,128]{2,1,0:T(8,128)(2,1)}, bf16[4,64,64]{2,1,0:T(8,128)(2,1)}) custom-call(s32[2,64]{1,0:T(2,128)} %bitcast.167, bf16[2,64]{1,0:T(2,128)(2,1)} %bitcast.168, bf16[48,64]{1,0:T(8,128)(2,1)} %bitcast.166), custom_call_target="tpu_custom_call" | custom-call | flops 4000000 | bytes 300000 | tf_op jit(solution)/shard_map/dispatch/pallas_call | solution.py:142
  1.9 56.5 %all_to_all.25 = bf16[32,8,128]{2,1,0:T(8,128)(2,1)S(1)} all-to-all(bf16[32,8,128]{2,1,0:T(8,128)(2,1)} %bitcast.155), channel_id=1, replica_groups=mesh['za'=4,'zb'=4,'x'=4,'y'=4,'zh'=2,'c'=2] {'za','y','zh'}, dimensions={0} | all-to-all | bytes 131072 | tf_op jit(solution)/shard_map/all_to_all | solution.py:19
  58.4 0.7 broadcast_in_dim.8
  59.1 4.6 %all-to-all-start.1 = ((bf16[4,256,128]{2,1,0:T(8,128)(2,1)}), bf16[4,256,128]{2,1,0:T(8,128)(2,1)S(1)}, u32[]{:S(2)}, u32[]{:S(2)}) async-start(bf16[4,256,128]{2,1,0:T(8,128)(2,1)} %broadcast_in_dim.8), calls=%async_computation.1 | async-start | bytes 524288 | tf_op jit(solution)/shard_map/all_to_all | solution.py:19
  63.8 0.4 copy.21
  64.2 0.5 copy-done.5
  64.7 0.6 fusion.45
  65.3 0.6 slice_bitcast_fusion.9
  66.1 3.9 %all-to-all-done.1 = bf16[4,256,128]{2,1,0:T(8,128)(2,1)S(1)} async-done(((bf16[4,256,128]{2,1,0:T(8,128)(2,1)}), bf16[4,256,128]{2,1,0:T(8,128)(2,1)S(1)}, u32[]{:S(2)}, u32[]{:S(2)}) %all-to-all-start.1) | async-done | bytes 262176 | tf_op jit(solution)/shard_map/all_to_all | solution.py:19
  70.0 0.7 copy-done
  70.7 1.9 %unpack.1 = bf16[160,768]{1,0:T(8,128)(2,1)} custom-call(bf16[4,4,64,128]{3,2,1,0:T(8,128)(2,1)} %bitcast.145), custom_call_target="tpu_custom_call" | custom-call | flops 4000000 | bytes 300000 | tf_op jit(solution)/shard_map/unpack/pallas_call | solution.py:142
  72.6 15.2 %all-gather = bf16[640,768]{1,0:T(8,128)(2,1)S(1)} all-gather(bf16[160,768]{1,0:T(8,128)(2,1)} %unpack.1), channel_id=2, replica_groups=mesh['za'=4,'zb'=4,'x'=4,'y'=4,'zh'=2,'c'=2] {'x'}, dimensions={0}, use_global_device_ids=true | all-gather | bytes 1228800 | tf_op jit(solution)/shard_map/all_gather | solution.py:177
  87.8 1.9 %collective-permute-start = (bf16[4,160,768]{2,1,0:T(8,128)(2,1)S(1)}, bf16[4,160,768]{2,1,0:T(8,128)(2,1)}, u32[]{:S(2)}, u32[]{:S(2)}) collective-permute-start(bf16[4,160,768]{2,1,0:T(8,128)(2,1)S(1)} %bitcast.123), channel_id=1, source_target_pairs={{0,1},{1,0},{2,3},{3,2},{4,5},{5,4},{6,7},{7,6},{8,9},{9,8},{10,11... | collective-permute-start | bytes 2949128 | tf_op jit(solution)/shard_map/ppermute | solution.py:23
  89.7 0.6 fusion.46
  90.4 0.2 fusion.24
  90.6 0.2 convolution_add_fusion.11
  90.8 0.2 convolution_add_fusion.10
  91.1 1.3 collective-permute-done
  92.4 1.1 fusion.19
  93.5 1.1 fusion.20
  94.7 1.2 fusion.18
  95.9 1.2 fusion.39
  97.1 0.2 fusion.33
  97.4 0.2 fusion.47
  97.6 0.2 fusion.48
  97.8 0.2 fusion.51
  98.0 0.2 fusion.52
  98.3 0.2 fusion.53
  98.5 0.2 fusion.54
  98.7 0.2 fusion.11
  99.0 0.2 fusion.10
  99.2 0.2 fusion.9
  99.4 0.2 fusion.8
  99.7 0.1 pad_maximum_fusion
  99.8 2.1 %collective-permute-start.1 = (bf16[4,160,768]{2,1,0:T(8,128)(2,1)S(1)}, bf16[4,160,768]{2,1,0:T(8,128)(2,1)S(1)}, u32[]{:S(2)}, u32[]{:S(2)}) collective-permute-start(bf16[4,160,768]{2,1,0:T(8,128)(2,1)S(1)} %pad_maximum_fusion), channel_id=1, source_target_pairs={{0,1},{1,0},{2,3},{3,2},{4,5},{5,4},{6,7},{7,6},{8,9},{9,8},{10,11... | collective-permute-start | bytes 2949128 | tf_op jit(solution)/shard_map/ppermute | solution.py:23
  101.9 0.2 fusion.15
  102.1 0.2 fusion.14
  102.3 0.2 fusion.49
  102.6 0.2 fusion.13
  102.8 0.2 fusion.50
  103.0 0.2 fusion.12
  103.3 1.0 collective-permute-done.1
  104.3 0.2 add_convert_fusion
  104.5 18.1 %all_to_all.26.in_ref = bf16[4,160,768]{2,1,0:T(8,128)(2,1)} all-to-all(bf16[4,160,768]{2,1,0:T(8,128)(2,1)S(1)} %add_convert_fusion), channel_id=1, replica_groups=mesh['za'=4,'zb'=4,'x'=4,'y'=4,'zh'=2,'c'=2] {'x'}, dimensions={0} | all-to-all | bytes 1966080 | tf_op jit(solution)/shard_map/all_to_all | solution.py:19
  122.6 2.3 %pack.1 = bf16[4,4,64,128]{3,2,1,0:T(8,128)(2,1)} custom-call(bf16[4,160,768]{2,1,0:T(8,128)(2,1)} %all_to_all.26.in_ref), custom_call_target="tpu_custom_call" | custom-call | flops 4000000 | bytes 300000 | tf_op jit(solution)/shard_map/pack/pallas_call | solution.py:142
  125.0 10.4 %all_to_all.27 = bf16[4,256,128]{2,1,0:T(8,128)(2,1)S(1)} all-to-all(bf16[4,256,128]{2,1,0:T(8,128)(2,1)} %bitcast.144), channel_id=1, replica_groups=mesh['za'=4,'zb'=4,'x'=4,'y'=4,'zh'=2,'c'=2] {'zb'}, dimensions={0} | all-to-all | bytes 524288 | tf_op jit(solution)/shard_map/all_to_all | solution.py:19
  135.4 31.2 %all_to_all.28 = bf16[32,8,128]{2,1,0:T(8,128)(2,1)} all-to-all(bf16[32,8,128]{2,1,0:T(8,128)(2,1)S(1)} %bitcast.152), channel_id=1, replica_groups=mesh['za'=4,'zb'=4,'x'=4,'y'=4,'zh'=2,'c'=2] {'za','y','zh'}, dimensions={0} | all-to-all | bytes 131072 | tf_op jit(solution)/shard_map/all_to_all | solution.py:19
  166.7 1.8 %pick.1 = bf16[48,64]{1,0:T(8,128)(2,1)} custom-call(bf16[4,64,128]{2,1,0:T(8,128)(2,1)} %bitcast.154, bf16[4,64,64]{2,1,0:T(8,128)(2,1)} %get-tuple-element.8.pick_ref), custom_call_target="tpu_custom_call" | custom-call | flops 4000000 | bytes 300000 | tf_op jit(solution)/shard_map/pick/pallas_call | solution.py:142
  (27 shorter events, 0.3 us)
Async XLA Ops:
  0.0 63.8 %copy-start.1 = (bf16[1,128,3072]{2,1,0:T(8,128)(2,1)S(1)}, bf16[1,128,3072]{2,1,0:T(8,128)(2,1)}, u32[]{:S(2)}) copy-start(bf16[1,128,3072]{2,1,0:T(8,128)(2,1)} %param.15) | copy-start | bytes 2359300
  59.1 5.0 %copy-start.4 = (bf16[1,320,128]{2,1,0:T(8,128)(2,1)S(1)}, bf16[1,320,128]{2,1,0:T(8,128)(2,1)}, u32[]{:S(2)}) copy-start(bf16[1,320,128]{2,1,0:T(8,128)(2,1)} %param.12) | copy-start | bytes 245764
  59.1 10.9 %all-to-all-start.1 = ((bf16[4,256,128]{2,1,0:T(8,128)(2,1)}), bf16[4,256,128]{2,1,0:T(8,128)(2,1)S(1)}, u32[]{:S(2)}, u32[]{:S(2)}) async-start(bf16[4,256,128]{2,1,0:T(8,128)(2,1)} %broadcast_in_dim.8), calls=%async_computation.1 | async-start | bytes 524288 | tf_op jit(solution)/shard_map/all_to_all | solution.py:19
  63.8 0.9 copy-start.5
  64.7 1.3 copy-start.2
  66.1 24.3 %copy-start.3 = (bf16[1,3072,128]{2,1,0:T(8,128)(2,1)S(1)}, bf16[1,3072,128]{2,1,0:T(8,128)(2,1)}, u32[]{:S(2)}) copy-start(bf16[1,3072,128]{2,1,0:T(8,128)(2,1)} %param.14) | copy-start | bytes 2359300
  70.0 0.7 copy-start
  87.8 4.6 %collective-permute-start = (bf16[4,160,768]{2,1,0:T(8,128)(2,1)S(1)}, bf16[4,160,768]{2,1,0:T(8,128)(2,1)}, u32[]{:S(2)}, u32[]{:S(2)}) collective-permute-start(bf16[4,160,768]{2,1,0:T(8,128)(2,1)S(1)} %bitcast.123), channel_id=1, source_target_pairs={{0,1},{1,0},{2,3},{3,2},{4,5},{5,4},{6,7},{7,6},{8,9},{9,8},{10,11... | collective-permute-start | bytes 2949128 | tf_op jit(solution)/shard_map/ppermute | solution.py:23
  90.8 5.0 %copy-start.6 = (bf16[64,128]{1,0:T(8,128)(2,1)S(1)}, bf16[64,128]{1,0:T(8,128)(2,1)}, u32[]{:S(2)}) copy-start(bf16[64,128]{1,0:T(8,128)(2,1)} %get-tuple-element.41) | copy-start | bytes 49156
  90.8 5.0 %copy-start.7 = (bf16[8,1,4,128]{3,2,1,0:T(4,128)(2,1)S(1)}, bf16[8,1,4,128]{3,2,1,0:T(4,128)(2,1)}, u32[]{:S(2)}) copy-start(bf16[8,1,4,128]{3,2,1,0:T(4,128)(2,1)} %get-tuple-element.25) | copy-start | bytes 24580
  90.8 5.0 %copy-start.8 = (bf16[8,1,4,128]{3,2,1,0:T(4,128)(2,1)S(1)}, bf16[8,1,4,128]{3,2,1,0:T(4,128)(2,1)}, u32[]{:S(2)}) copy-start(bf16[8,1,4,128]{3,2,1,0:T(4,128)(2,1)} %get-tuple-element.26) | copy-start | bytes 24580
  90.8 5.0 %copy-start.9 = (bf16[8,1,4,128]{3,2,1,0:T(4,128)(2,1)S(1)}, bf16[8,1,4,128]{3,2,1,0:T(4,128)(2,1)}, u32[]{:S(2)}) copy-start(bf16[8,1,4,128]{3,2,1,0:T(4,128)(2,1)} %get-tuple-element.31) | copy-start | bytes 24580
  90.8 5.0 %copy-start.10 = (bf16[8,1,4,128]{3,2,1,0:T(4,128)(2,1)S(1)}, bf16[8,1,4,128]{3,2,1,0:T(4,128)(2,1)}, u32[]{:S(2)}) copy-start(bf16[8,1,4,128]{3,2,1,0:T(4,128)(2,1)} %get-tuple-element.32) | copy-start | bytes 24580
  99.8 4.5 %collective-permute-start.1 = (bf16[4,160,768]{2,1,0:T(8,128)(2,1)S(1)}, bf16[4,160,768]{2,1,0:T(8,128)(2,1)S(1)}, u32[]{:S(2)}, u32[]{:S(2)}) collective-permute-start(bf16[4,160,768]{2,1,0:T(8,128)(2,1)S(1)} %pad_maximum_fusion), channel_id=1, source_target_pairs={{0,1},{1,0},{2,3},{3,2},{4,5},{5,4},{6,7},{7,6},{8,9},{9,8},{10,11... | collective-permute-start | bytes 2949128 | tf_op jit(solution)/shard_map/ppermute | solution.py:23

commit v4 on v3

--- a/solution.py
+++ b/solution.py
@@ -136,16 +136,62 @@
     out_ref[...] = out.astype(BF16)
 
 
-def call(kernel, name, out, *args):
-    shapes = [jax.ShapeDtypeStruct(s, BF16) for s in out]
+def weights_kernel(
+    cap, core_ref, down_ref, gate_ref, up_ref, gates_ref, ups_ref, down_out, both_out, pre_out, turned
+):
+    nx, nz, width, hid = down_out.shape
+    features = nx * nz * width
+    for at in range(0, features, 128):
+        to = min(at + 128, features)
+        turned[at:to, :] = down_ref[:, at:to].T
+    for z in range(nz):
+        for x in range(nx):
+            at = (z * nx + x) * width
+            down_out[x, z] = turned[at : at + width, :]
+            both_out[x, z, :, :hid] = gate_ref[at : at + width, :]
+            both_out[x, z, :, hid:] = up_ref[at : at + width, :]
+    slots = gates_ref.shape[0]
+    half = slots // 2
+    eight = half // cap * 8
+    row, source = counted((half, slots), 0), counted((half, slots), 1)
+    rest = row - 2 * eight
+    block = jnp.where(row < 2 * eight, (row & (eight - 1)) >> 3, rest >> 2)
+    slot = jnp.where(row < eight, row & 7, jnp.where(row < 2 * eight, 8 + (row & 7), 16 + (rest & 3)))
+    for other in range(2):
+        core = core_ref[0] if other == 0 else 1 - core_ref[0]
+        picks = (source == (block * 2 + core) * cap + slot).astype(F32).astype(BF16)
+        pre_out[other, 0] = jnp.dot(picks, gates_ref[...], preferred_element_type=F32).astype(BF16)
+        pre_out[other, 1] = jnp.dot(picks, ups_ref[...], preferred_element_type=F32).astype(BF16)
+
+
+def through_kernel(other, rows_ref, down_ref, both_ref, pre_ref, out_ref):
+    nx = rows_ref.shape[0]
+    projected = jnp.dot(rows_ref[0], down_ref[0], preferred_element_type=F32)
+    for k in range(1, nx):
+        projected = projected + jnp.dot(rows_ref[k], down_ref[k], preferred_element_type=F32)
+    gate_pre = pre_ref[other, 0].astype(F32)
+    up_pre = pre_ref[other, 1].astype(F32)
+    sig = jax.nn.sigmoid(gate_pre)
+    gate_grad = (projected * up_pre * sig * (1.0 + gate_pre * (1.0 - sig))).astype(BF16)
+    up_grad = (projected * gate_pre * sig).astype(BF16)
+    both = jnp.concatenate([gate_grad, up_grad], axis=1)
+    for k in range(nx):
+        out_ref[k] = times_t(both, both_ref[k]).astype(out_ref.dtype)
+
+
+def call(kernel, name, out, *args, dtype=BF16, scratch=(), flops=4000000):
+    shapes = [jax.ShapeDtypeStruct(s, dtype) for s in out]
     whole = pl.BlockSpec(memory_space=pltpu.VMEM)
+    scalars = pl.BlockSpec(memory_space=pltpu.SMEM)
     return pl.pallas_call(
         kernel,
         name=name,
         out_shape=shapes,
-        in_specs=[whole] * len(args),
+        in_specs=[scalars if a.ndim == 1 else whole for a in args],
         out_specs=[whole] * len(out),
-        cost_estimate=pl.CostEstimate(flops=4000000, bytes_accessed=300000, transcendentals=0),
+        scratch_shapes=scratch,
+        compiler_params=pltpu.CompilerParams(vmem_limit_bytes=8 << 20),
+        cost_estimate=pl.CostEstimate(flops=flops, bytes_accessed=300000, transcendentals=0),
     )(*args)
 
 
@@ -160,7 +206,6 @@
     span = na * nb * width
     rows = experts * 8
     assert cap == 20 and 2 * width + width // 2 <= 128
-    first_core = lax.axis_index("c") == 0
 
     sent, picks = call(
         dispatch_kernel,
@@ -171,49 +216,49 @@
         out_grad.T,
     )
     got = exchange(sent.reshape(na * experts, 8, 128), FAR)
+    got, w_down = lax.optimization_barrier((got, w_down))
+
+    features = nx * span
+    nz = na * nb
+    down, both, pre = call(
+        functools.partial(weights_kernel, cap),
+        "weights",
+        [(nx, nz, width, hid), (nx, nz, width, 2 * hid), (2, 2, half, hid)],
+        lax.axis_index("c").astype(jnp.int32).reshape(1),
+        w_down[0],
+        w_gate[0],
+        w_up[0],
+        saved_gate[0],
+        saved_up[0],
+        scratch=[pltpu.VMEM((features, hid), BF16)],
+        flops=100000000,
+    )
+    down = down.reshape(nx, span, hid)
+    both = both.reshape(nx, span, 2 * hid)
     got = jnp.broadcast_to(got.reshape(1, na * rows, 128), (nb, na * rows, 128))
     got = exchange(got, "zb").reshape(nb, na, rows, 128)
+    got, down, both, pre = lax.optimization_barrier((got, down, both, pre))
     (got,) = call(functools.partial(unpack_kernel, width), "unpack", [(half, span)], got)
     own_rows = lax.all_gather(got, "x")
     other_rows = swap(own_rows)
 
-    down = w_down[0].reshape(hid, na * nb, nx, width).transpose(2, 0, 1, 3).reshape(nx, hid, span)
-    gate_w = w_gate[0].reshape(na * nb, nx, width, hid).transpose(1, 0, 2, 3).reshape(nx, span, hid)
-    up_w = w_up[0].reshape(na * nb, nx, width, hid).transpose(1, 0, 2, 3).reshape(nx, span, hid)
-
-    def by_core(a):
-        parts = a[0].reshape(experts, nc, cap, hid)
-        parts = jnp.stack(
-            [
-                jnp.concatenate(
-                    [parts[:, k, at:to].reshape(-1, hid) for at, to in ((0, 8), (8, 16), (16, cap))]
-                )
-                for k in range(nc)
-            ]
+    def through(rows, other, dtype):
+        (out,) = call(
+            functools.partial(through_kernel, other),
+            ("own", "other")[other],
+            [(nx, half, span)],
+            rows,
+            down,
+            both,
+            pre,
+            dtype=dtype,
+            flops=2 * half * features * hid * 3,
         )
-        return (
-            jnp.where(first_core, parts[0], parts[1]).astype(F32),
-            jnp.where(first_core, parts[1], parts[0]).astype(F32),
-        )
-
-    gates = by_core(saved_gate)
-    ups = by_core(saved_up)
-
-    def through(rows, gate_pre, up_pre):
-        projected = sum(times_t(rows[k], down[k]) for k in range(nx))
-        sig = jax.nn.sigmoid(gate_pre)
-        gate_grad = (projected * up_pre * sig * (1.0 + gate_pre * (1.0 - sig))).astype(BF16)
-        up_grad = (projected * gate_pre * sig).astype(BF16)
-        return jnp.stack(
-            [
-                (times_t(gate_grad, gate_w[k]) + times_t(up_grad, up_w[k])).astype(BF16)
-                for k in range(nx)
-            ]
-        )
-
-    for_other = through(other_rows, gates[1], ups[1])
-    for_own = through(own_rows, gates[0], ups[0])
-    shares = (for_own.astype(F32) + swap(for_other).astype(F32)).astype(BF16)
+        return out
+
+    for_own = through(own_rows, 0, F32)
+    for_other = through(other_rows, 1, BF16)
+    shares = (for_own + swap(for_other).astype(F32)).astype(BF16)
     shares = exchange(shares, "x")
     (back,) = call(functools.partial(pack_kernel, width), "pack", [(nb, na, rows, 128)], shares)
     back = exchange(back.reshape(nb, na * rows, 128), "zb")

time: 169 us -> 156 us (0.923)
  matrix products: 9.06 us -> 0 us
  local copies, waits for them, and re-layouts: 4.34 us -> 7.95 us
  Pallas kernels: 7.9 us -> 4.62 us
  waiting for transfers between devices: 6.22 us -> 4.34 us
    dot_general x24 -> x0, matrix products: 9.06 us -> none  [times_t(): lax.dot_general(a, b, (((1,), (1,)), ((), ())), preferred_element_type=F32)]
    unnamed x23 -> x16, local copies, waits for them, and re-layouts: 1.58 us -> 7.21 us
    all_to_all x1, waiting for transfers between devices: 3.93 us -> 0.37 us  [exchange(): return lax.all_to_all(tiles, axes, split_axis=0, concat_axis=0, tiled=True)]
    pallas_call x4 -> x7, Pallas kernels: 7.9 us -> 4.62 us  [call(): pl.pallas_call(kernel, name=name, out_shape=shapes, in_specs=[scalars if...]
    all_to_all x4, blocking collectives: 116 us -> 114 us  [exchange(): return lax.all_to_all(tiles, axes, split_axis=0, concat_axis=0, tiled=True)]
  transfers between devices with their start and end apart: 3 -> 3, of which waited for: 3 -> 3; matrix products, arithmetic and copies ran while one was open for 3% -> 0% of each run, Pallas kernels for 0% -> 1%
where the time goes in v4:
time: 156 us
  blocking collectives  130 us (83%)
  starting transfers between devices  8.46 us (5%)
  local copies, waits for them, and re-layouts  7.95 us (5%)
  Pallas kernels  4.62 us (3%)
  waiting for transfers between devices  4.34 us (3%)
    all_to_all x4, blocking collectives, exchange(): return lax.all_to_all(tiles, axes, split_axis=0, concat_axis=0, tiled=True)  114 us
    all_gather x1, blocking collectives, local(): own_rows = lax.all_gather(got, 'x')  15.4 us
    unnamed x16, local copies, waits for them, and re-layouts  7.21 us
    pallas_call x7, Pallas kernels, call(): pl.pallas_call(kernel, name=name, out_shape=shapes, in_specs=[scalars if...  4.62 us
    all_to_all x1, starting transfers between devices, exchange(): return lax.all_to_all(tiles, axes, split_axis=0, concat_axis=0, tiled=True)  4.51 us
    ppermute x2, waiting for transfers between devices, swap(): return lax.ppermute(value, 'c', [(0, 1), (1, 0)])  3.97 us
    ppermute x2, starting transfers between devices, swap(): return lax.ppermute(value, 'c', [(0, 1), (1, 0)])  3.95 us
  transfers between devices with their start and end apart: 3, of which 3 were waited for; matrix products, arithmetic and copies ran while one was open for 0% of the time, Pallas kernels for 1%

profile of v4, /device:TPU:32, one launch (start us, length us, event | category | flops | bytes accessed | tf_op | source)
XLA Modules:
  0.0 155.5 jit_solution(9527105112459341708)
XLA Ops:
  0.0 0.0 copy-start.5
  0.0 0.7 copy-done.5
  0.7 0.0 copy-start.6
  0.7 0.7 copy-done.6
  1.4 0.0 copy-start.7
  1.4 0.7 copy-done.7
  2.0 0.4 dispatch.1
  2.5 56.3 %all_to_all.25 = bf16[32,8,128]{2,1,0:T(8,128)(2,1)S(1)} all-to-all(bf16[32,8,128]{2,1,0:T(8,128)(2,1)S(1)} %bitcast.33), channel_id=1, replica_groups=mesh['za'=4,'zb'=4,'x'=4,'y'=4,'zh'=2,'c'=2] {'za','y','zh'}, dimensions={0} | all-to-all | bytes 131072 | tf_op jit(solution)/shard_map/all_to_all | solution.py:19
  58.8 0.7 broadcast_in_dim.8
  59.5 4.5 %all-to-all-start.1 = ((bf16[4,256,128]{2,1,0:T(8,128)(2,1)}), bf16[4,256,128]{2,1,0:T(8,128)(2,1)S(1)}, u32[]{:S(2)}, u32[]{:S(2)}) async-start(bf16[4,256,128]{2,1,0:T(8,128)(2,1)} %broadcast_in_dim.8), calls=%async_computation.1 | async-start | bytes 524288 | tf_op jit(solution)/shard_map/all_to_all | solution.py:19
  64.1 0.0 copy-start
  64.1 1.1 copy-done
  65.2 0.0 copy-start.1
  65.2 1.1 copy-done.1
  66.3 0.0 copy-start.2
  66.3 1.1 copy-done.2
  67.5 0.0 copy-start.3
  67.5 0.9 copy-done.3
  68.3 0.0 copy-start.4
  68.3 0.9 copy-done.4
  69.2 0.7 weights.1
  69.9 0.4 all-to-all-done.1
  70.3 0.3 unpack.1
  70.6 15.4 %all-gather = bf16[640,768]{1,0:T(8,128)(2,1)S(1)} all-gather(bf16[160,768]{1,0:T(8,128)(2,1)S(1)} %unpack.1), channel_id=2, replica_groups=mesh['za'=4,'zb'=4,'x'=4,'y'=4,'zh'=2,'c'=2] {'x'}, dimensions={0}, use_global_device_ids=true | all-gather | bytes 1228800 | tf_op jit(solution)/shard_map/all_gather | solution.py:242
  85.9 1.9 %collective-permute-start = (bf16[4,160,768]{2,1,0:T(8,128)(2,1)S(1)}, bf16[4,160,768]{2,1,0:T(8,128)(2,1)S(1)}, u32[]{:S(2)}, u32[]{:S(2)}) collective-permute-start(bf16[4,160,768]{2,1,0:T(8,128)(2,1)S(1)} %bitcast.21), channel_id=1, source_target_pairs={{0,1},{1,0},{2,3},{3,2},{4,5},{5,4},{6,7},{7,6},{8,9},{9,8},{10,11... | collective-permute-start | bytes 2949128 | tf_op jit(solution)/shard_map/ppermute | solution.py:23
  87.9 2.5 %collective-permute-done.rows_ref = bf16[4,160,768]{2,1,0:T(8,128)(2,1)S(1)} collective-permute-done((bf16[4,160,768]{2,1,0:T(8,128)(2,1)S(1)}, bf16[4,160,768]{2,1,0:T(8,128)(2,1)S(1)}, u32[]{:S(2)}, u32[]{:S(2)}) %collective-permute-start) | collective-permute-done | bytes 983072 | tf_op jit(solution)/shard_map/ppermute | solution.py:23
  90.4 1.0 other.1
  91.4 2.0 %collective-permute-start.1 = (bf16[4,160,768]{2,1,0:T(8,128)(2,1)S(1)}, bf16[4,160,768]{2,1,0:T(8,128)(2,1)S(1)}, u32[]{:S(2)}, u32[]{:S(2)}) collective-permute-start(bf16[4,160,768]{2,1,0:T(8,128)(2,1)S(1)} %other.1), channel_id=1, source_target_pairs={{0,1},{1,0},{2,3},{3,2},{4,5},{5,4},{6,7},{7,6},{8,9},{9,8},{10,11... | collective-permute-start | bytes 2949128 | tf_op jit(solution)/shard_map/ppermute | solution.py:23
  93.4 1.0 own.1
  94.4 1.4 collective-permute-done.1
  95.8 0.2 add_convert_fusion
  96.1 17.4 %all_to_all.26.in_ref = bf16[4,160,768]{2,1,0:T(8,128)(2,1)S(1)} all-to-all(bf16[4,160,768]{2,1,0:T(8,128)(2,1)S(1)} %add_convert_fusion), channel_id=1, replica_groups=mesh['za'=4,'zb'=4,'x'=4,'y'=4,'zh'=2,'c'=2] {'x'}, dimensions={0} | all-to-all | bytes 1966080 | tf_op jit(solution)/shard_map/all_to_all | solution.py:19
  113.4 0.4 pack.1
  113.8 10.8 %all_to_all.27 = bf16[4,256,128]{2,1,0:T(8,128)(2,1)S(1)} all-to-all(bf16[4,256,128]{2,1,0:T(8,128)(2,1)S(1)} %bitcast.25), channel_id=1, replica_groups=mesh['za'=4,'zb'=4,'x'=4,'y'=4,'zh'=2,'c'=2] {'zb'}, dimensions={0} | all-to-all | bytes 524288 | tf_op jit(solution)/shard_map/all_to_all | solution.py:19
  124.6 30.0 %all_to_all.28 = bf16[32,8,128]{2,1,0:T(8,128)(2,1)S(1)} all-to-all(bf16[32,8,128]{2,1,0:T(8,128)(2,1)S(1)} %bitcast.37), channel_id=1, replica_groups=mesh['za'=4,'zb'=4,'x'=4,'y'=4,'zh'=2,'c'=2] {'za','y','zh'}, dimensions={0} | all-to-all | bytes 131072 | tf_op jit(solution)/shard_map/all_to_all | solution.py:19
  154.6 0.9 pick.1
  (1 shorter events, 0.0 us)
Async XLA Ops:
  0.0 0.7 copy-start.5
  0.7 0.7 copy-start.6
  1.4 0.7 copy-start.7
  59.5 10.7 %all-to-all-start.1 = ((bf16[4,256,128]{2,1,0:T(8,128)(2,1)}), bf16[4,256,128]{2,1,0:T(8,128)(2,1)S(1)}, u32[]{:S(2)}, u32[]{:S(2)}) async-start(bf16[4,256,128]{2,1,0:T(8,128)(2,1)} %broadcast_in_dim.8), calls=%async_computation.1 | async-start | bytes 524288 | tf_op jit(solution)/shard_map/all_to_all | solution.py:19
  64.1 1.1 copy-start
  65.2 1.1 copy-start.1
  66.3 1.1 copy-start.2
  67.5 0.9 copy-start.3
  68.3 0.9 copy-start.4
  85.9 4.4 %collective-permute-start = (bf16[4,160,768]{2,1,0:T(8,128)(2,1)S(1)}, bf16[4,160,768]{2,1,0:T(8,128)(2,1)S(1)}, u32[]{:S(2)}, u32[]{:S(2)}) collective-permute-start(bf16[4,160,768]{2,1,0:T(8,128)(2,1)S(1)} %bitcast.21), channel_id=1, source_target_pairs={{0,1},{1,0},{2,3},{3,2},{4,5},{5,4},{6,7},{7,6},{8,9},{9,8},{10,11... | collective-permute-start | bytes 2949128 | tf_op jit(solution)/shard_map/ppermute | solution.py:23
  91.4 4.5 %collective-permute-start.1 = (bf16[4,160,768]{2,1,0:T(8,128)(2,1)S(1)}, bf16[4,160,768]{2,1,0:T(8,128)(2,1)S(1)}, u32[]{:S(2)}, u32[]{:S(2)}) collective-permute-start(bf16[4,160,768]{2,1,0:T(8,128)(2,1)S(1)} %other.1), channel_id=1, source_target_pairs={{0,1},{1,0},{2,3},{3,2},{4,5},{5,4},{6,7},{7,6},{8,9},{9,8},{10,11... | collective-permute-start | bytes 2949128 | tf_op jit(solution)/shard_map/ppermute | solution.py:23

commit v5 on v4

--- a/solution.py
+++ b/solution.py
@@ -45,23 +45,23 @@
     return hit.astype(F32).astype(BF16)
 
 
-def dispatch_kernel(ids_ref, prob_ref, grad_ref, tile_ref, pick_ref):
+def dispatch_kernel(width, in_ref, tile_ref, pick_ref):
     copies, rows, _ = tile_ref.shape
-    width, tokens = grad_ref.shape
+    tokens = in_ref.shape[1]
+    routing = in_ref[width:, :].astype(F32)
     expert = counted((rows, tokens), 0) >> 3
     row = counted((rows, tokens), 0) & 7
-    first = ids_ref[0:1, :] == expert
-    second = ids_ref[1:2, :] == expert
+    first = routing[0:1, :].astype(jnp.int32) == expert
+    second = routing[1:2, :].astype(jnp.int32) == expert
     named = first | second
-    prob = prob_ref[...].astype(F32)
-    weight = jnp.where(first, prob[0:1, :], 0.0) + jnp.where(second, prob[1:2, :], 0.0)
+    weight = jnp.where(first, routing[2:3, :], 0.0) + jnp.where(second, routing[3:4, :], 0.0)
     earlier = counted((tokens, tokens), 0) < counted((tokens, tokens), 1)
     slot = jnp.dot(
         named.astype(F32).astype(BF16),
         earlier.astype(F32).astype(BF16),
         preferred_element_type=F32,
     ).astype(jnp.int32)
-    grad = grad_ref[...]
+    grad = in_ref[:width, :]
     total = jnp.zeros((rows, 128), F32)
     for part in range(PARTS):
         hit = named & (slot == row + (0, 8, 16, 12)[part])
@@ -136,10 +136,8 @@
     out_ref[...] = out.astype(BF16)
 
 
-def weights_kernel(
-    cap, core_ref, down_ref, gate_ref, up_ref, gates_ref, ups_ref, down_out, both_out, pre_out, turned
-):
-    nx, nz, width, hid = down_out.shape
+def weights_kernel(cap, core_ref, down_ref, saved_ref, down_out, pre_out, turned):
+    nx, nz, width, _ = down_out.shape
     features = nx * nz * width
     for at in range(0, features, 128):
         to = min(at + 128, features)
@@ -148,9 +146,7 @@
         for x in range(nx):
             at = (z * nx + x) * width
             down_out[x, z] = turned[at : at + width, :]
-            both_out[x, z, :, :hid] = gate_ref[at : at + width, :]
-            both_out[x, z, :, hid:] = up_ref[at : at + width, :]
-    slots = gates_ref.shape[0]
+    slots = saved_ref.shape[1]
     half = slots // 2
     eight = half // cap * 8
     row, source = counted((half, slots), 0), counted((half, slots), 1)
@@ -160,8 +156,9 @@
     for other in range(2):
         core = core_ref[0] if other == 0 else 1 - core_ref[0]
         picks = (source == (block * 2 + core) * cap + slot).astype(F32).astype(BF16)
-        pre_out[other, 0] = jnp.dot(picks, gates_ref[...], preferred_element_type=F32).astype(BF16)
-        pre_out[other, 1] = jnp.dot(picks, ups_ref[...], preferred_element_type=F32).astype(BF16)
+        for kind in range(2):
+            mine = jnp.dot(picks, saved_ref[kind], preferred_element_type=F32)
+            pre_out[other, kind] = mine.astype(BF16)
 
 
 def through_kernel(other, rows_ref, down_ref, both_ref, pre_ref, out_ref):
@@ -176,7 +173,8 @@
     up_grad = (projected * gate_pre * sig).astype(BF16)
     both = jnp.concatenate([gate_grad, up_grad], axis=1)
     for k in range(nx):
-        out_ref[k] = times_t(both, both_ref[k]).astype(out_ref.dtype)
+        weights = both_ref[:, k].reshape(out_ref.shape[2], both.shape[1])
+        out_ref[k] = times_t(both, weights).astype(out_ref.dtype)
 
 
 def call(kernel, name, out, *args, dtype=BF16, scratch=(), flops=4000000):
@@ -208,33 +206,34 @@
     assert cap == 20 and 2 * width + width // 2 <= 128
 
     sent, picks = call(
-        dispatch_kernel,
+        functools.partial(dispatch_kernel, width),
         "dispatch",
         [(na, rows, 128), (PARTS, rows, tokens)],
-        expert_ids.T,
-        gate_probs.T,
-        out_grad.T,
+        jnp.pad(
+            jnp.concatenate([out_grad.T, expert_ids.T.astype(BF16), gate_probs.T]),
+            ((0, -(width + 4) % 16), (0, 0)),
+        ),
     )
     got = exchange(sent.reshape(na * experts, 8, 128), FAR)
-    got, w_down = lax.optimization_barrier((got, w_down))
+    got, w_down, w_gate, w_up, saved_gate, saved_up = lax.optimization_barrier(
+        (got, w_down, w_gate, w_up, saved_gate, saved_up)
+    )
 
     features = nx * span
     nz = na * nb
-    down, both, pre = call(
+    nz = na * nb
+    both = jnp.concatenate([w_gate[0], w_up[0]], axis=1).reshape(nz, nx, width, 2 * hid)
+    down, pre = call(
         functools.partial(weights_kernel, cap),
         "weights",
-        [(nx, nz, width, hid), (nx, nz, width, 2 * hid), (2, 2, half, hid)],
+        [(nx, nz, width, hid), (2, 2, half, hid)],
         lax.axis_index("c").astype(jnp.int32).reshape(1),
         w_down[0],
-        w_gate[0],
-        w_up[0],
-        saved_gate[0],
-        saved_up[0],
+        jnp.concatenate([saved_gate, saved_up]),
         scratch=[pltpu.VMEM((features, hid), BF16)],
         flops=100000000,
     )
     down = down.reshape(nx, span, hid)
-    both = both.reshape(nx, span, 2 * hid)
     got = jnp.broadcast_to(got.reshape(1, na * rows, 128), (nb, na * rows, 128))
     got = exchange(got, "zb").reshape(nb, na, rows, 128)
     got, down, both, pre = lax.optimization_barrier((got, down, both, pre))

time: 156 us -> 155 us (level)
  local copies, waits for them, and re-layouts: 7.95 us -> 1.85 us
  other arithmetic: 0.27 us -> 4.21 us
  waiting for transfers between devices: 4.34 us -> 6.12 us
    unnamed x16 -> x2, local copies, waits for them, and re-layouts: 7.21 us -> 1.13 us
    concatenate x0 -> x3, other arithmetic: none -> 3.25 us  [the longest x1 1.58 us: local(): jnp.concatenate([w_gate[0], w_up[0]], axis=1)]
    all_to_all x1, waiting for transfers between devices: 0.37 us -> 2.16 us  [exchange(): return lax.all_to_all(tiles, axes, split_axis=0, concat_axis=0, tiled=True)]
  transfers between devices with their start and end apart: 3 -> 3, of which waited for: 3 -> 3; matrix products, arithmetic and copies ran while one was open for 0% -> 2% of each run, Pallas kernels for 1% -> 1%
where the time goes in v5:
time: 155 us
  blocking collectives  130 us (84%)
  starting transfers between devices  8.47 us (5%)
  waiting for transfers between devices  6.12 us (4%)
  Pallas kernels  4.34 us (3%)
  other arithmetic  4.21 us (3%)
  local copies, waits for them, and re-layouts  1.85 us (1%)
    all_to_all x4, blocking collectives, exchange(): return lax.all_to_all(tiles, axes, split_axis=0, concat_axis=0, tiled=True)  115 us
    all_gather x1, blocking collectives, local(): own_rows = lax.all_gather(got, 'x')  15 us
    all_to_all x1, starting transfers between devices, exchange(): return lax.all_to_all(tiles, axes, split_axis=0, concat_axis=0, tiled=True)  4.51 us
    pallas_call x7, Pallas kernels, call(): pl.pallas_call(kernel, name=name, out_shape=shapes, in_specs=[scalars if...  4.34 us
    ppermute x2, waiting for transfers between devices, swap(): return lax.ppermute(value, 'c', [(0, 1), (1, 0)])  3.96 us
    ppermute x2, starting transfers between devices, swap(): return lax.ppermute(value, 'c', [(0, 1), (1, 0)])  3.96 us
  transfers between devices with their start and end apart: 3, of which 3 were waited for; matrix products, arithmetic and copies ran while one was open for 2% of the time, Pallas kernels for 1%

profile of v5, /device:TPU:32, one launch (start us, length us, event | category | flops | bytes accessed | tf_op | source)
XLA Modules:
  0.0 154.9 jit_solution(6535663637008610794)
XLA Ops:
  0.0 0.7 convert_bitcast_fusion
  0.7 0.7 fusion.4.in_ref
  1.4 0.4 dispatch.1
  1.8 56.3 %all_to_all.25 = bf16[32,8,128]{2,1,0:T(8,128)(2,1)S(1)} all-to-all(bf16[32,8,128]{2,1,0:T(8,128)(2,1)S(1)} %bitcast.25), channel_id=1, replica_groups=mesh['za'=4,'zb'=4,'x'=4,'y'=4,'zh'=2,'c'=2] {'za','y','zh'}, dimensions={0} | all-to-all | bytes 131072 | tf_op jit(solution)/shard_map/all_to_all | solution.py:19
  58.2 0.7 broadcast_in_dim.8
  58.9 4.5 %all-to-all-start.1 = ((bf16[4,256,128]{2,1,0:T(8,128)(2,1)}), bf16[4,256,128]{2,1,0:T(8,128)(2,1)S(1)}, u32[]{:S(2)}, u32[]{:S(2)}) async-start(bf16[4,256,128]{2,1,0:T(8,128)(2,1)} %broadcast_in_dim.8), calls=%async_computation.1 | async-start | bytes 524288 | tf_op jit(solution)/shard_map/all_to_all | solution.py:19
  63.4 0.9 pad_maximum_fusion.1.saved_ref
  64.4 0.0 copy-start
  64.4 1.1 copy-done
  65.5 0.4 weights.1
  65.9 1.6 %pad_maximum_fusion.both_ref = bf16[16,4,48,256]{3,2,1,0:T(8,128)(2,1)S(1)} fusion(bf16[16,4,48,128]{3,2,1,0:T(8,128)(2,1)} %bitcast.26, bf16[16,4,48,128]{3,2,1,0:T(8,128)(2,1)} %bitcast.27), kind=kLoop, calls=%fused_computation.1 | loop fusion | flops 3145728 | bytes 3145728 | tf_op jit(solution)/shard_map/concatenate | solution.py:225
  67.5 2.2 %all-to-all-done.1 = bf16[4,256,128]{2,1,0:T(8,128)(2,1)S(1)} async-done(((bf16[4,256,128]{2,1,0:T(8,128)(2,1)}), bf16[4,256,128]{2,1,0:T(8,128)(2,1)S(1)}, u32[]{:S(2)}, u32[]{:S(2)}) %all-to-all-start.1) | async-done | bytes 262176 | tf_op jit(solution)/shard_map/all_to_all | solution.py:19
  69.6 0.3 unpack.1
  69.9 15.0 %all-gather = bf16[640,768]{1,0:T(8,128)(2,1)S(1)} all-gather(bf16[160,768]{1,0:T(8,128)(2,1)S(1)} %unpack.1), channel_id=2, replica_groups=mesh['za'=4,'zb'=4,'x'=4,'y'=4,'zh'=2,'c'=2] {'x'}, dimensions={0}, use_global_device_ids=true | all-gather | bytes 1228800 | tf_op jit(solution)/shard_map/all_gather | solution.py:241
  84.9 1.9 %collective-permute-start = (bf16[4,160,768]{2,1,0:T(8,128)(2,1)S(1)}, bf16[4,160,768]{2,1,0:T(8,128)(2,1)S(1)}, u32[]{:S(2)}, u32[]{:S(2)}) collective-permute-start(bf16[4,160,768]{2,1,0:T(8,128)(2,1)S(1)} %bitcast.17), channel_id=1, source_target_pairs={{0,1},{1,0},{2,3},{3,2},{4,5},{5,4},{6,7},{7,6},{8,9},{9,8},{10,11... | collective-permute-start | bytes 2949128 | tf_op jit(solution)/shard_map/ppermute | solution.py:23
  86.8 2.5 %collective-permute-done.rows_ref = bf16[4,160,768]{2,1,0:T(8,128)(2,1)S(1)} collective-permute-done((bf16[4,160,768]{2,1,0:T(8,128)(2,1)S(1)}, bf16[4,160,768]{2,1,0:T(8,128)(2,1)S(1)}, u32[]{:S(2)}, u32[]{:S(2)}) %collective-permute-start) | collective-permute-done | bytes 983072 | tf_op jit(solution)/shard_map/ppermute | solution.py:23
  89.3 1.0 other.1
  90.3 2.0 %collective-permute-start.1 = (bf16[4,160,768]{2,1,0:T(8,128)(2,1)S(1)}, bf16[4,160,768]{2,1,0:T(8,128)(2,1)S(1)}, u32[]{:S(2)}, u32[]{:S(2)}) collective-permute-start(bf16[4,160,768]{2,1,0:T(8,128)(2,1)S(1)} %other.1), channel_id=1, source_target_pairs={{0,1},{1,0},{2,3},{3,2},{4,5},{5,4},{6,7},{7,6},{8,9},{9,8},{10,11... | collective-permute-start | bytes 2949128 | tf_op jit(solution)/shard_map/ppermute | solution.py:23
  92.4 1.0 own.1
  93.3 1.4 collective-permute-done.1
  94.8 0.2 add_convert_fusion
  95.0 18.0 %all_to_all.26.in_ref = bf16[4,160,768]{2,1,0:T(8,128)(2,1)S(1)} all-to-all(bf16[4,160,768]{2,1,0:T(8,128)(2,1)S(1)} %add_convert_fusion), channel_id=1, replica_groups=mesh['za'=4,'zb'=4,'x'=4,'y'=4,'zh'=2,'c'=2] {'x'}, dimensions={0} | all-to-all | bytes 1966080 | tf_op jit(solution)/shard_map/all_to_all | solution.py:19
  113.0 0.4 pack.1
  113.4 10.0 %all_to_all.27 = bf16[4,256,128]{2,1,0:T(8,128)(2,1)S(1)} all-to-all(bf16[4,256,128]{2,1,0:T(8,128)(2,1)S(1)} %bitcast.21), channel_id=1, replica_groups=mesh['za'=4,'zb'=4,'x'=4,'y'=4,'zh'=2,'c'=2] {'zb'}, dimensions={0} | all-to-all | bytes 524288 | tf_op jit(solution)/shard_map/all_to_all | solution.py:19
  123.5 30.5 %all_to_all.28 = bf16[32,8,128]{2,1,0:T(8,128)(2,1)S(1)} all-to-all(bf16[32,8,128]{2,1,0:T(8,128)(2,1)S(1)} %bitcast.28), channel_id=1, replica_groups=mesh['za'=4,'zb'=4,'x'=4,'y'=4,'zh'=2,'c'=2] {'za','y','zh'}, dimensions={0} | all-to-all | bytes 131072 | tf_op jit(solution)/shard_map/all_to_all | solution.py:19
  154.0 0.9 pick.1
  (1 shorter events, 0.0 us)
Async XLA Ops:
  58.9 10.7 %all-to-all-start.1 = ((bf16[4,256,128]{2,1,0:T(8,128)(2,1)}), bf16[4,256,128]{2,1,0:T(8,128)(2,1)S(1)}, u32[]{:S(2)}, u32[]{:S(2)}) async-start(bf16[4,256,128]{2,1,0:T(8,128)(2,1)} %broadcast_in_dim.8), calls=%async_computation.1 | async-start | bytes 524288 | tf_op jit(solution)/shard_map/all_to_all | solution.py:19
  64.4 1.1 copy-start
  84.9 4.4 %collective-permute-start = (bf16[4,160,768]{2,1,0:T(8,128)(2,1)S(1)}, bf16[4,160,768]{2,1,0:T(8,128)(2,1)S(1)}, u32[]{:S(2)}, u32[]{:S(2)}) collective-permute-start(bf16[4,160,768]{2,1,0:T(8,128)(2,1)S(1)} %bitcast.17), channel_id=1, source_target_pairs={{0,1},{1,0},{2,3},{3,2},{4,5},{5,4},{6,7},{7,6},{8,9},{9,8},{10,11... | collective-permute-start | bytes 2949128 | tf_op jit(solution)/shard_map/ppermute | solution.py:23
  90.3 4.5 %collective-permute-start.1 = (bf16[4,160,768]{2,1,0:T(8,128)(2,1)S(1)}, bf16[4,160,768]{2,1,0:T(8,128)(2,1)S(1)}, u32[]{:S(2)}, u32[]{:S(2)}) collective-permute-start(bf16[4,160,768]{2,1,0:T(8,128)(2,1)S(1)} %other.1), channel_id=1, source_target_pairs={{0,1},{1,0},{2,3},{3,2},{4,5},{5,4},{6,7},{7,6},{8,9},{9,8},{10,11... | collective-permute-start | bytes 2949128 | tf_op jit(solution)/shard_map/ppermute | solution.py:23

commit v6 on v5

--- a/solution.py
+++ b/solution.py
@@ -45,23 +45,23 @@
     return hit.astype(F32).astype(BF16)
 
 
-def dispatch_kernel(width, in_ref, tile_ref, pick_ref):
+def dispatch_kernel(ids_ref, prob_ref, grad_ref, tile_ref, pick_ref):
     copies, rows, _ = tile_ref.shape
-    tokens = in_ref.shape[1]
-    routing = in_ref[width:, :].astype(F32)
+    width, tokens = grad_ref.shape
     expert = counted((rows, tokens), 0) >> 3
     row = counted((rows, tokens), 0) & 7
-    first = routing[0:1, :].astype(jnp.int32) == expert
-    second = routing[1:2, :].astype(jnp.int32) == expert
+    first = ids_ref[0:1, :] == expert
+    second = ids_ref[1:2, :] == expert
     named = first | second
-    weight = jnp.where(first, routing[2:3, :], 0.0) + jnp.where(second, routing[3:4, :], 0.0)
+    prob = prob_ref[...].astype(F32)
+    weight = jnp.where(first, prob[0:1, :], 0.0) + jnp.where(second, prob[1:2, :], 0.0)
     earlier = counted((tokens, tokens), 0) < counted((tokens, tokens), 1)
     slot = jnp.dot(
         named.astype(F32).astype(BF16),
         earlier.astype(F32).astype(BF16),
         preferred_element_type=F32,
     ).astype(jnp.int32)
-    grad = in_ref[:width, :]
+    grad = grad_ref[...]
     total = jnp.zeros((rows, 128), F32)
     for part in range(PARTS):
         hit = named & (slot == row + (0, 8, 16, 12)[part])
@@ -177,7 +177,7 @@
         out_ref[k] = times_t(both, weights).astype(out_ref.dtype)
 
 
-def call(kernel, name, out, *args, dtype=BF16, scratch=(), flops=4000000):
+def call(kernel, name, out, *args, dtype=BF16, scratch=(), flops=4000000, grant=8):
     shapes = [jax.ShapeDtypeStruct(s, dtype) for s in out]
     whole = pl.BlockSpec(memory_space=pltpu.VMEM)
     scalars = pl.BlockSpec(memory_space=pltpu.SMEM)
@@ -188,7 +188,7 @@
         in_specs=[scalars if a.ndim == 1 else whole for a in args],
         out_specs=[whole] * len(out),
         scratch_shapes=scratch,
-        compiler_params=pltpu.CompilerParams(vmem_limit_bytes=8 << 20),
+        compiler_params=pltpu.CompilerParams(vmem_limit_bytes=grant << 20),
         cost_estimate=pl.CostEstimate(flops=flops, bytes_accessed=300000, transcendentals=0),
     )(*args)
 
@@ -206,21 +206,19 @@
     assert cap == 20 and 2 * width + width // 2 <= 128
 
     sent, picks = call(
-        functools.partial(dispatch_kernel, width),
+        dispatch_kernel,
         "dispatch",
         [(na, rows, 128), (PARTS, rows, tokens)],
-        jnp.pad(
-            jnp.concatenate([out_grad.T, expert_ids.T.astype(BF16), gate_probs.T]),
-            ((0, -(width + 4) % 16), (0, 0)),
-        ),
-    )
-    got = exchange(sent.reshape(na * experts, 8, 128), FAR)
-    got, w_down, w_gate, w_up, saved_gate, saved_up = lax.optimization_barrier(
-        (got, w_down, w_gate, w_up, saved_gate, saved_up)
+        expert_ids.T,
+        gate_probs.T,
+        out_grad.T,
+        grant=60,
+    )
+    sent, w_down, w_gate, w_up, saved_gate, saved_up = lax.optimization_barrier(
+        (sent, w_down, w_gate, w_up, saved_gate, saved_up)
     )
 
     features = nx * span
-    nz = na * nb
     nz = na * nb
     both = jnp.concatenate([w_gate[0], w_up[0]], axis=1).reshape(nz, nx, width, 2 * hid)
     down, pre = call(
@@ -234,9 +232,10 @@
         flops=100000000,
     )
     down = down.reshape(nx, span, hid)
+    got = exchange(sent.reshape(na * experts, 8, 128), FAR)
+    got, down, both, pre = lax.optimization_barrier((got, down, both, pre))
     got = jnp.broadcast_to(got.reshape(1, na * rows, 128), (nb, na * rows, 128))
     got = exchange(got, "zb").reshape(nb, na, rows, 128)
-    got, down, both, pre = lax.optimization_barrier((got, down, both, pre))
     (got,) = call(functools.partial(unpack_kernel, width), "unpack", [(half, span)], got)
     own_rows = lax.all_gather(got, "x")
     other_rows = swap(own_rows)

time: 155 us -> 155 us (level)
  blocking collectives: 130 us -> 84.1 us
  starting transfers between devices: 8.47 us -> 34.4 us
  waiting for transfers between devices: 6.12 us -> 26 us
    all_to_all x4, blocking collectives: 115 us -> 68.7 us  [exchange(): return lax.all_to_all(tiles, axes, split_axis=0, concat_axis=0, tiled=True)]
    all_to_all x1, starting transfers between devices: 4.51 us -> 30.5 us  [exchange(): return lax.all_to_all(tiles, axes, split_axis=0, concat_axis=0, tiled=True)]
    all_to_all x1, waiting for transfers between devices: 2.16 us -> 22 us  [exchange(): return lax.all_to_all(tiles, axes, split_axis=0, concat_axis=0, tiled=True)]
where the time goes in v6:
time: 155 us; the launch traced here: 154 us
  blocking collectives  84.1 us (54%)
  starting transfers between devices  34.4 us (22%)
  waiting for transfers between devices  26 us (17%)
  Pallas kernels  5.71 us (4%)
  other arithmetic  2.8 us (2%)
    all_to_all x4, blocking collectives, exchange(): return lax.all_to_all(tiles, axes, split_axis=0, concat_axis=0, tiled=True)  68.7 us
    all_to_all x1, starting transfers between devices, exchange(): return lax.all_to_all(tiles, axes, split_axis=0, concat_axis=0, tiled=True)  30.5 us
    all_to_all x1, waiting for transfers between devices, exchange(): return lax.all_to_all(tiles, axes, split_axis=0, concat_axis=0, tiled=True)  22 us
    all_gather x1, blocking collectives, local(): own_rows = lax.all_gather(got, 'x')  15.4 us
    pallas_call x7, Pallas kernels, call(): pl.pallas_call(kernel, name=name, out_shape=shapes, in_specs=[scalars if...  5.71 us
    ppermute x2, waiting for transfers between devices, swap(): return lax.ppermute(value, 'c', [(0, 1), (1, 0)])  3.96 us
    ppermute x2, starting transfers between devices, swap(): return lax.ppermute(value, 'c', [(0, 1), (1, 0)])  3.95 us
  transfers between devices with their start and end apart: 3, of which 3 were waited for; matrix products, arithmetic and copies ran while one was open for 2% of the time, Pallas kernels for 1%

profile of v6, /device:TPU:32, one launch (start us, length us, event | category | flops | bytes accessed | tf_op | source)
XLA Modules:
  0.0 154.3 jit_solution(391121705545179319)
XLA Ops:
  0.0 1.8 %dispatch.1 = (bf16[4,64,128]{2,1,0:T(8,128)(2,1)}, bf16[4,64,64]{2,1,0:T(8,128)(2,1)}) custom-call(s32[2,64]{1,0:T(2,128)} %bitcast.30, bf16[2,64]{1,0:T(2,128)(2,1)} %bitcast.31, bf16[48,64]{1,0:T(8,128)(2,1)} %bitcast.29), custom_call_target="tpu_custom_call" | custom-call | flops 4000000 | bytes 300000 | tf_op jit(solution)/shard_map/dispatch/pallas_call | solution.py:184
  1.8 30.5 %all-to-all-start = ((bf16[32,8,128]{2,1,0:T(8,128)(2,1)}), bf16[32,8,128]{2,1,0:T(8,128)(2,1)S(1)}, u32[]{:S(2)}, u32[]{:S(2)}) async-start(bf16[32,8,128]{2,1,0:T(8,128)(2,1)} %bitcast.28), calls=%async_computation | async-start | bytes 131072 | tf_op jit(solution)/shard_map/all_to_all | solution.py:19
  32.3 0.9 pad_maximum_fusion.1.saved_ref
  33.2 0.0 copy-start
  33.2 1.1 copy-done
  34.3 0.4 weights.1
  34.7 1.6 %pad_maximum_fusion.both_ref = bf16[16,4,48,256]{3,2,1,0:T(8,128)(2,1)S(1)} fusion(bf16[16,4,48,128]{3,2,1,0:T(8,128)(2,1)} %bitcast.24, bf16[16,4,48,128]{3,2,1,0:T(8,128)(2,1)} %bitcast.25), kind=kLoop, calls=%fused_computation.1 | loop fusion | flops 3145728 | bytes 3145728 | tf_op jit(solution)/shard_map/concatenate | solution.py:223
  36.3 22.0 %all-to-all-done = bf16[32,8,128]{2,1,0:T(8,128)(2,1)S(1)} async-done(((bf16[32,8,128]{2,1,0:T(8,128)(2,1)}), bf16[32,8,128]{2,1,0:T(8,128)(2,1)S(1)}, u32[]{:S(2)}, u32[]{:S(2)}) %all-to-all-start) | async-done | bytes 65568 | tf_op jit(solution)/shard_map/all_to_all | solution.py:19
  58.4 10.5 %all_to_all.25 = bf16[4,256,128]{2,1,0:T(8,128)(2,1)S(1)} all-to-all(bf16[4,256,128]{2,1,0:T(8,128)(2,1)S(1)} %broadcast_in_dim.8), channel_id=1, replica_groups=mesh['za'=4,'zb'=4,'x'=4,'y'=4,'zh'=2,'c'=2] {'zb'}, dimensions={0} | all-to-all | bytes 524288 | tf_op jit(solution)/shard_map/all_to_all | solution.py:19
  68.9 0.3 unpack.1
  69.2 15.4 %all-gather = bf16[640,768]{1,0:T(8,128)(2,1)S(1)} all-gather(bf16[160,768]{1,0:T(8,128)(2,1)S(1)} %unpack.1), channel_id=2, replica_groups=mesh['za'=4,'zb'=4,'x'=4,'y'=4,'zh'=2,'c'=2] {'x'}, dimensions={0}, use_global_device_ids=true | all-gather | bytes 1228800 | tf_op jit(solution)/shard_map/all_gather | solution.py:240
  84.6 1.9 %collective-permute-start = (bf16[4,160,768]{2,1,0:T(8,128)(2,1)S(1)}, bf16[4,160,768]{2,1,0:T(8,128)(2,1)S(1)}, u32[]{:S(2)}, u32[]{:S(2)}) collective-permute-start(bf16[4,160,768]{2,1,0:T(8,128)(2,1)S(1)} %bitcast.16), channel_id=1, source_target_pairs={{0,1},{1,0},{2,3},{3,2},{4,5},{5,4},{6,7},{7,6},{8,9},{9,8},{10,11... | collective-permute-start | bytes 2949128 | tf_op jit(solution)/shard_map/ppermute | solution.py:23
  86.5 2.5 %collective-permute-done.rows_ref = bf16[4,160,768]{2,1,0:T(8,128)(2,1)S(1)} collective-permute-done((bf16[4,160,768]{2,1,0:T(8,128)(2,1)S(1)}, bf16[4,160,768]{2,1,0:T(8,128)(2,1)S(1)}, u32[]{:S(2)}, u32[]{:S(2)}) %collective-permute-start) | collective-permute-done | bytes 983072 | tf_op jit(solution)/shard_map/ppermute | solution.py:23
  89.0 1.0 other.1
  90.0 2.0 %collective-permute-start.1 = (bf16[4,160,768]{2,1,0:T(8,128)(2,1)S(1)}, bf16[4,160,768]{2,1,0:T(8,128)(2,1)S(1)}, u32[]{:S(2)}, u32[]{:S(2)}) collective-permute-start(bf16[4,160,768]{2,1,0:T(8,128)(2,1)S(1)} %other.1), channel_id=1, source_target_pairs={{0,1},{1,0},{2,3},{3,2},{4,5},{5,4},{6,7},{7,6},{8,9},{9,8},{10,11... | collective-permute-start | bytes 2949128 | tf_op jit(solution)/shard_map/ppermute | solution.py:23
  92.0 1.0 own.1
  93.0 1.4 collective-permute-done.1
  94.4 0.2 add_convert_fusion
  94.7 0.0 copy-start.1
  94.7 18.3 %all_to_all.26.in_ref = bf16[4,160,768]{2,1,0:T(8,128)(2,1)S(1)} all-to-all(bf16[4,160,768]{2,1,0:T(8,128)(2,1)S(1)} %add_convert_fusion), channel_id=1, replica_groups=mesh['za'=4,'zb'=4,'x'=4,'y'=4,'zh'=2,'c'=2] {'x'}, dimensions={0} | all-to-all | bytes 1966080 | tf_op jit(solution)/shard_map/all_to_all | solution.py:19
  113.0 0.4 pack.1
  113.4 9.8 %all_to_all.27 = bf16[4,256,128]{2,1,0:T(8,128)(2,1)S(1)} all-to-all(bf16[4,256,128]{2,1,0:T(8,128)(2,1)S(1)} %bitcast.20), channel_id=1, replica_groups=mesh['za'=4,'zb'=4,'x'=4,'y'=4,'zh'=2,'c'=2] {'zb'}, dimensions={0} | all-to-all | bytes 524288 | tf_op jit(solution)/shard_map/all_to_all | solution.py:19
  123.2 30.1 %all_to_all.28 = bf16[32,8,128]{2,1,0:T(8,128)(2,1)S(1)} all-to-all(bf16[32,8,128]{2,1,0:T(8,128)(2,1)S(1)} %bitcast.27), channel_id=1, replica_groups=mesh['za'=4,'zb'=4,'x'=4,'y'=4,'zh'=2,'c'=2] {'za','y','zh'}, dimensions={0} | all-to-all | bytes 131072 | tf_op jit(solution)/shard_map/all_to_all | solution.py:19
  153.3 0.0 copy-done.1
  153.3 0.9 pick.1
  (2 shorter events, 0.1 us)
Async XLA Ops:
  1.8 56.5 %all-to-all-start = ((bf16[32,8,128]{2,1,0:T(8,128)(2,1)}), bf16[32,8,128]{2,1,0:T(8,128)(2,1)S(1)}, u32[]{:S(2)}, u32[]{:S(2)}) async-start(bf16[32,8,128]{2,1,0:T(8,128)(2,1)} %bitcast.28), calls=%async_computation | async-start | bytes 131072 | tf_op jit(solution)/shard_map/all_to_all | solution.py:19
  33.2 1.1 copy-start
  84.6 4.4 %collective-permute-start = (bf16[4,160,768]{2,1,0:T(8,128)(2,1)S(1)}, bf16[4,160,768]{2,1,0:T(8,128)(2,1)S(1)}, u32[]{:S(2)}, u32[]{:S(2)}) collective-permute-start(bf16[4,160,768]{2,1,0:T(8,128)(2,1)S(1)} %bitcast.16), channel_id=1, source_target_pairs={{0,1},{1,0},{2,3},{3,2},{4,5},{5,4},{6,7},{7,6},{8,9},{9,8},{10,11... | collective-permute-start | bytes 2949128 | tf_op jit(solution)/shard_map/ppermute | solution.py:23
  90.0 4.5 %collective-permute-start.1 = (bf16[4,160,768]{2,1,0:T(8,128)(2,1)S(1)}, bf16[4,160,768]{2,1,0:T(8,128)(2,1)S(1)}, u32[]{:S(2)}, u32[]{:S(2)}) collective-permute-start(bf16[4,160,768]{2,1,0:T(8,128)(2,1)S(1)} %other.1), channel_id=1, source_target_pairs={{0,1},{1,0},{2,3},{3,2},{4,5},{5,4},{6,7},{7,6},{8,9},{9,8},{10,11... | collective-permute-start | bytes 2949128 | tf_op jit(solution)/shard_map/ppermute | solution.py:23
  94.7 58.7 %copy-start.1 = (bf16[4,64,64]{2,1,0:T(8,128)(2,1)S(1)}, bf16[4,64,64]{2,1,0:T(8,128)(2,1)}, u32[]{:S(2)}) copy-start(bf16[4,64,64]{2,1,0:T(8,128)(2,1)} %get-tuple-element.32.pick_ref) | copy-start | bytes 98308

commit v7 on v6

--- a/solution.py
+++ b/solution.py
@@ -136,7 +136,9 @@
     out_ref[...] = out.astype(BF16)
 
 
-def weights_kernel(cap, core_ref, down_ref, saved_ref, down_out, pre_out, turned):
+def weights_kernel(
+    cap, core_ref, down_ref, gate_ref, up_ref, saved_ref, down_out, both_out, pre_out, turned, block
+):
     nx, nz, width, _ = down_out.shape
     features = nx * nz * width
     for at in range(0, features, 128):
@@ -146,6 +148,15 @@
         for x in range(nx):
             at = (z * nx + x) * width
             down_out[x, z] = turned[at : at + width, :]
+    span, hid = nz * width, both_out.shape[1] // 2
+    for kind, ref in enumerate((gate_ref, up_ref)):
+        for x in range(nx):
+            for z in range(nz):
+                at = (z * nx + x) * width
+                block[z * width : (z + 1) * width, :] = ref[at : at + width, :]
+            for at in range(0, span, 128):
+                to = min(at + 128, span)
+                both_out[x, kind * hid : (kind + 1) * hid, at:to] = block[at:to, :].T
     slots = saved_ref.shape[1]
     half = slots // 2
     eight = half // cap * 8
@@ -173,8 +184,8 @@
     up_grad = (projected * gate_pre * sig).astype(BF16)
     both = jnp.concatenate([gate_grad, up_grad], axis=1)
     for k in range(nx):
-        weights = both_ref[:, k].reshape(out_ref.shape[2], both.shape[1])
-        out_ref[k] = times_t(both, weights).astype(out_ref.dtype)
+        share = jnp.dot(both, both_ref[k], preferred_element_type=F32)
+        out_ref[k] = share.astype(out_ref.dtype)
 
 
 def call(kernel, name, out, *args, dtype=BF16, scratch=(), flops=4000000, grant=8):
@@ -220,15 +231,16 @@
 
     features = nx * span
     nz = na * nb
-    both = jnp.concatenate([w_gate[0], w_up[0]], axis=1).reshape(nz, nx, width, 2 * hid)
-    down, pre = call(
+    down, both, pre = call(
         functools.partial(weights_kernel, cap),
         "weights",
-        [(nx, nz, width, hid), (2, 2, half, hid)],
+        [(nx, nz, width, hid), (nx, 2 * hid, span), (2, 2, half, hid)],
         lax.axis_index("c").astype(jnp.int32).reshape(1),
         w_down[0],
+        w_gate[0],
+        w_up[0],
         jnp.concatenate([saved_gate, saved_up]),
-        scratch=[pltpu.VMEM((features, hid), BF16)],
+        scratch=[pltpu.VMEM((features, hid), BF16), pltpu.VMEM((span, hid), BF16)],
         flops=100000000,
     )
     down = down.reshape(nx, span, hid)

time: 155 us -> 155 us (level)
  local copies, waits for them, and re-layouts: 1.17 us -> 3.43 us
  other arithmetic: 2.8 us -> 1.22 us
    unnamed x4 -> x8, local copies, waits for them, and re-layouts: 1.13 us -> 3.4 us
    concatenate x1 -> x0, other arithmetic: 1.58 us -> none  [local(): jnp.concatenate([w_gate[0], w_up[0]], axis=1)]
  transfers between devices with their start and end apart: 3 -> 3, of which waited for: 3 -> 3; matrix products, arithmetic and copies ran while one was open for 2% -> 1% of each run, Pallas kernels for 1% -> 1%
where the time goes in v7:
time: 155 us; the launch traced here: 154 us
  blocking collectives  84.1 us (54%)
  starting transfers between devices  34.4 us (22%)
  waiting for transfers between devices  25.1 us (16%)
  Pallas kernels  5.71 us (4%)
  local copies, waits for them, and re-layouts  3.43 us (2%)
    all_to_all x4, blocking collectives, exchange(): return lax.all_to_all(tiles, axes, split_axis=0, concat_axis=0, tiled=True)  68.7 us
    all_to_all x1, starting transfers between devices, exchange(): return lax.all_to_all(tiles, axes, split_axis=0, concat_axis=0, tiled=True)  30.5 us
    all_to_all x1, waiting for transfers between devices, exchange(): return lax.all_to_all(tiles, axes, split_axis=0, concat_axis=0, tiled=True)  20.9 us
    all_gather x1, blocking collectives, local(): own_rows = lax.all_gather(got, 'x')  15.4 us
    pallas_call x7, Pallas kernels, call(): pl.pallas_call(kernel, name=name, out_shape=shapes, in_specs=[scalars if...  5.71 us
    ppermute x2, waiting for transfers between devices, swap(): return lax.ppermute(value, 'c', [(0, 1), (1, 0)])  4.17 us
    ppermute x2, starting transfers between devices, swap(): return lax.ppermute(value, 'c', [(0, 1), (1, 0)])  3.95 us
    unnamed x8, local copies, waits for them, and re-layouts  3.4 us
  transfers between devices with their start and end apart: 3, of which 3 were waited for; matrix products, arithmetic and copies ran while one was open for 1% of the time, Pallas kernels for 1%

profile of v7, /device:TPU:32, one launch (start us, length us, event | category | flops | bytes accessed | tf_op | source)
XLA Modules:
  0.0 154.1 jit_solution(11401456328902377727)
XLA Ops:
  0.0 1.8 %dispatch.1 = (bf16[4,64,128]{2,1,0:T(8,128)(2,1)}, bf16[4,64,64]{2,1,0:T(8,128)(2,1)}) custom-call(s32[2,64]{1,0:T(2,128)} %bitcast.30, bf16[2,64]{1,0:T(2,128)(2,1)} %bitcast.31, bf16[48,64]{1,0:T(8,128)(2,1)} %bitcast.29), custom_call_target="tpu_custom_call" | custom-call | flops 4000000 | bytes 300000 | tf_op jit(solution)/shard_map/dispatch/pallas_call | solution.py:195
  1.8 30.5 %all-to-all-start = ((bf16[32,8,128]{2,1,0:T(8,128)(2,1)}), bf16[32,8,128]{2,1,0:T(8,128)(2,1)S(1)}, u32[]{:S(2)}, u32[]{:S(2)}) async-start(bf16[32,8,128]{2,1,0:T(8,128)(2,1)} %bitcast.28), calls=%async_computation | async-start | bytes 131072 | tf_op jit(solution)/shard_map/all_to_all | solution.py:19
  32.3 0.9 pad_maximum_fusion.saved_ref
  33.2 0.0 copy-start
  33.2 1.1 copy-done
  34.4 0.0 copy-start.1
  34.4 1.1 copy-done.1
  35.5 0.0 copy-start.2
  35.5 1.1 copy-done.2
  36.6 0.8 weights.1
  37.4 20.9 %all-to-all-done = bf16[32,8,128]{2,1,0:T(8,128)(2,1)S(1)} async-done(((bf16[32,8,128]{2,1,0:T(8,128)(2,1)}), bf16[32,8,128]{2,1,0:T(8,128)(2,1)S(1)}, u32[]{:S(2)}, u32[]{:S(2)}) %all-to-all-start) | async-done | bytes 65568 | tf_op jit(solution)/shard_map/all_to_all | solution.py:19
  58.4 10.5 %all_to_all.25 = bf16[4,256,128]{2,1,0:T(8,128)(2,1)S(1)} all-to-all(bf16[4,256,128]{2,1,0:T(8,128)(2,1)S(1)} %broadcast_in_dim.8), channel_id=1, replica_groups=mesh['za'=4,'zb'=4,'x'=4,'y'=4,'zh'=2,'c'=2] {'zb'}, dimensions={0} | all-to-all | bytes 524288 | tf_op jit(solution)/shard_map/all_to_all | solution.py:19
  68.9 0.3 unpack.1
  69.2 15.4 %all-gather = bf16[640,768]{1,0:T(8,128)(2,1)S(1)} all-gather(bf16[160,768]{1,0:T(8,128)(2,1)S(1)} %unpack.1), channel_id=2, replica_groups=mesh['za'=4,'zb'=4,'x'=4,'y'=4,'zh'=2,'c'=2] {'x'}, dimensions={0}, use_global_device_ids=true | all-gather | bytes 1228800 | tf_op jit(solution)/shard_map/all_gather | solution.py:252
  84.6 1.9 %collective-permute-start = (bf16[4,160,768]{2,1,0:T(8,128)(2,1)S(1)}, bf16[4,160,768]{2,1,0:T(8,128)(2,1)S(1)}, u32[]{:S(2)}, u32[]{:S(2)}) collective-permute-start(bf16[4,160,768]{2,1,0:T(8,128)(2,1)S(1)} %bitcast.16), channel_id=1, source_target_pairs={{0,1},{1,0},{2,3},{3,2},{4,5},{5,4},{6,7},{7,6},{8,9},{9,8},{10,11... | collective-permute-start | bytes 2949128 | tf_op jit(solution)/shard_map/ppermute | solution.py:23
  86.5 2.5 %collective-permute-done.rows_ref = bf16[4,160,768]{2,1,0:T(8,128)(2,1)S(1)} collective-permute-done((bf16[4,160,768]{2,1,0:T(8,128)(2,1)S(1)}, bf16[4,160,768]{2,1,0:T(8,128)(2,1)S(1)}, u32[]{:S(2)}, u32[]{:S(2)}) %collective-permute-start) | collective-permute-done | bytes 983072 | tf_op jit(solution)/shard_map/ppermute | solution.py:23
  89.0 0.8 other.1
  89.8 2.0 %collective-permute-start.1 = (bf16[4,160,768]{2,1,0:T(8,128)(2,1)S(1)}, bf16[4,160,768]{2,1,0:T(8,128)(2,1)S(1)}, u32[]{:S(2)}, u32[]{:S(2)}) collective-permute-start(bf16[4,160,768]{2,1,0:T(8,128)(2,1)S(1)} %other.1), channel_id=1, source_target_pairs={{0,1},{1,0},{2,3},{3,2},{4,5},{5,4},{6,7},{7,6},{8,9},{9,8},{10,11... | collective-permute-start | bytes 2949128 | tf_op jit(solution)/shard_map/ppermute | solution.py:23
  91.8 0.8 own.1
  92.6 1.6 %collective-permute-done.1 = bf16[4,160,768]{2,1,0:T(8,128)(2,1)S(1)} collective-permute-done((bf16[4,160,768]{2,1,0:T(8,128)(2,1)S(1)}, bf16[4,160,768]{2,1,0:T(8,128)(2,1)S(1)}, u32[]{:S(2)}, u32[]{:S(2)}) %collective-permute-start.1) | collective-permute-done | bytes 983072 | tf_op jit(solution)/shard_map/ppermute | solution.py:23
  94.2 0.2 add_convert_fusion
  94.5 0.0 copy-start.3
  94.5 18.3 %all_to_all.26.in_ref = bf16[4,160,768]{2,1,0:T(8,128)(2,1)S(1)} all-to-all(bf16[4,160,768]{2,1,0:T(8,128)(2,1)S(1)} %add_convert_fusion), channel_id=1, replica_groups=mesh['za'=4,'zb'=4,'x'=4,'y'=4,'zh'=2,'c'=2] {'x'}, dimensions={0} | all-to-all | bytes 1966080 | tf_op jit(solution)/shard_map/all_to_all | solution.py:19
  112.8 0.4 pack.1
  113.2 9.8 %all_to_all.27 = bf16[4,256,128]{2,1,0:T(8,128)(2,1)S(1)} all-to-all(bf16[4,256,128]{2,1,0:T(8,128)(2,1)S(1)} %bitcast.20), channel_id=1, replica_groups=mesh['za'=4,'zb'=4,'x'=4,'y'=4,'zh'=2,'c'=2] {'zb'}, dimensions={0} | all-to-all | bytes 524288 | tf_op jit(solution)/shard_map/all_to_all | solution.py:19
  123.0 30.1 %all_to_all.28 = bf16[32,8,128]{2,1,0:T(8,128)(2,1)S(1)} all-to-all(bf16[32,8,128]{2,1,0:T(8,128)(2,1)S(1)} %bitcast.27), channel_id=1, replica_groups=mesh['za'=4,'zb'=4,'x'=4,'y'=4,'zh'=2,'c'=2] {'za','y','zh'}, dimensions={0} | all-to-all | bytes 131072 | tf_op jit(solution)/shard_map/all_to_all | solution.py:19
  153.1 0.0 copy-done.3
  153.1 0.9 pick.1
  (2 shorter events, 0.1 us)
Async XLA Ops:
  1.8 56.5 %all-to-all-start = ((bf16[32,8,128]{2,1,0:T(8,128)(2,1)}), bf16[32,8,128]{2,1,0:T(8,128)(2,1)S(1)}, u32[]{:S(2)}, u32[]{:S(2)}) async-start(bf16[32,8,128]{2,1,0:T(8,128)(2,1)} %bitcast.28), calls=%async_computation | async-start | bytes 131072 | tf_op jit(solution)/shard_map/all_to_all | solution.py:19
  33.2 1.1 copy-start
  34.4 1.1 copy-start.1
  35.5 1.1 copy-start.2
  84.6 4.4 %collective-permute-start = (bf16[4,160,768]{2,1,0:T(8,128)(2,1)S(1)}, bf16[4,160,768]{2,1,0:T(8,128)(2,1)S(1)}, u32[]{:S(2)}, u32[]{:S(2)}) collective-permute-start(bf16[4,160,768]{2,1,0:T(8,128)(2,1)S(1)} %bitcast.16), channel_id=1, source_target_pairs={{0,1},{1,0},{2,3},{3,2},{4,5},{5,4},{6,7},{7,6},{8,9},{9,8},{10,11... | collective-permute-start | bytes 2949128 | tf_op jit(solution)/shard_map/ppermute | solution.py:23
  89.8 4.5 %collective-permute-start.1 = (bf16[4,160,768]{2,1,0:T(8,128)(2,1)S(1)}, bf16[4,160,768]{2,1,0:T(8,128)(2,1)S(1)}, u32[]{:S(2)}, u32[]{:S(2)}) collective-permute-start(bf16[4,160,768]{2,1,0:T(8,128)(2,1)S(1)} %other.1), channel_id=1, source_target_pairs={{0,1},{1,0},{2,3},{3,2},{4,5},{5,4},{6,7},{7,6},{8,9},{9,8},{10,11... | collective-permute-start | bytes 2949128 | tf_op jit(solution)/shard_map/ppermute | solution.py:23
  94.5 58.7 %copy-start.3 = (bf16[4,64,64]{2,1,0:T(8,128)(2,1)S(1)}, bf16[4,64,64]{2,1,0:T(8,128)(2,1)}, u32[]{:S(2)}) copy-start(bf16[4,64,64]{2,1,0:T(8,128)(2,1)} %get-tuple-element.34.pick_ref) | copy-start | bytes 98308

commit v8 on v7

--- a/solution.py
+++ b/solution.py
@@ -273,7 +273,9 @@
     (back,) = call(functools.partial(pack_kernel, width), "pack", [(nb, na, rows, 128)], shares)
     back = exchange(back.reshape(nb, na * rows, 128), "zb")
     back = jnp.sum(back.astype(F32), axis=0).astype(BF16)
-    back = exchange(back.reshape(na * experts, 8, 128), FAR).reshape(na, rows, 128)
+    back = back.reshape(na, ny, nh, 8, 128).transpose(2, 0, 1, 3, 4)
+    back = exchange(back.reshape(na * experts, 8, 128), ("zh", "za", "y"))
+    back = back.reshape(nh, na, ny, 8, 128).transpose(1, 2, 0, 3, 4).reshape(na, rows, 128)
     (out,) = call(final_kernel, "pick", [(width, tokens)], back, picks)
     return out.T
 

time: 155 us -> 155 us (level)
  no operation moved by 1% of the time
where the time goes in v8:
time: 155 us
  blocking collectives  84.8 us (55%)
  starting transfers between devices  34.4 us (22%)
  waiting for transfers between devices  25.1 us (16%)
  Pallas kernels  5.71 us (4%)
  local copies, waits for them, and re-layouts  3.46 us (2%)
    all_to_all x4, blocking collectives, exchange(): return lax.all_to_all(tiles, axes, split_axis=0, concat_axis=0, tiled=True)  69.4 us
    all_to_all x1, starting transfers between devices, exchange(): return lax.all_to_all(tiles, axes, split_axis=0, concat_axis=0, tiled=True)  30.5 us
    all_to_all x1, waiting for transfers between devices, exchange(): return lax.all_to_all(tiles, axes, split_axis=0, concat_axis=0, tiled=True)  20.9 us
    all_gather x1, blocking collectives, local(): own_rows = lax.all_gather(got, 'x')  15.4 us
    pallas_call x7, Pallas kernels, call(): pl.pallas_call(kernel, name=name, out_shape=shapes, in_specs=[scalars if...  5.71 us
    ppermute x2, waiting for transfers between devices, swap(): return lax.ppermute(value, 'c', [(0, 1), (1, 0)])  4.17 us
    ppermute x2, starting transfers between devices, swap(): return lax.ppermute(value, 'c', [(0, 1), (1, 0)])  3.95 us
    unnamed x8, local copies, waits for them, and re-layouts  3.4 us
  transfers between devices with their start and end apart: 3, of which 3 were waited for; matrix products, arithmetic and copies ran while one was open for 1% of the time, Pallas kernels for 1%

profile of v8, /device:TPU:32, one launch (start us, length us, event | category | flops | bytes accessed | tf_op | source)
XLA Modules:
  0.0 154.8 jit_solution(8638669143766813246)
XLA Ops:
  0.0 1.8 %dispatch.1 = (bf16[4,64,128]{2,1,0:T(8,128)(2,1)}, bf16[4,64,64]{2,1,0:T(8,128)(2,1)}) custom-call(s32[2,64]{1,0:T(2,128)} %bitcast.38, bf16[2,64]{1,0:T(2,128)(2,1)} %bitcast.39, bf16[48,64]{1,0:T(8,128)(2,1)} %bitcast.37), custom_call_target="tpu_custom_call" | custom-call | flops 4000000 | bytes 300000 | tf_op jit(solution)/shard_map/dispatch/pallas_call | solution.py:195
  1.8 30.5 %all-to-all-start = ((bf16[32,8,128]{2,1,0:T(8,128)(2,1)}), bf16[32,8,128]{2,1,0:T(8,128)(2,1)S(1)}, u32[]{:S(2)}, u32[]{:S(2)}) async-start(bf16[32,8,128]{2,1,0:T(8,128)(2,1)} %bitcast.36), calls=%async_computation | async-start | bytes 131072 | tf_op jit(solution)/shard_map/all_to_all | solution.py:19
  32.3 0.9 pad_maximum_fusion.saved_ref
  33.2 0.0 copy-start
  33.2 1.1 copy-done
  34.4 0.0 copy-start.1
  34.4 1.1 copy-done.1
  35.5 0.0 copy-start.2
  35.5 1.1 copy-done.2
  36.6 0.8 weights.1
  37.4 20.9 %all-to-all-done = bf16[32,8,128]{2,1,0:T(8,128)(2,1)S(1)} async-done(((bf16[32,8,128]{2,1,0:T(8,128)(2,1)}), bf16[32,8,128]{2,1,0:T(8,128)(2,1)S(1)}, u32[]{:S(2)}, u32[]{:S(2)}) %all-to-all-start) | async-done | bytes 65568 | tf_op jit(solution)/shard_map/all_to_all | solution.py:19
  58.4 10.5 %all_to_all.25 = bf16[4,256,128]{2,1,0:T(8,128)(2,1)S(1)} all-to-all(bf16[4,256,128]{2,1,0:T(8,128)(2,1)S(1)} %broadcast_in_dim.8), channel_id=1, replica_groups=mesh['za'=4,'zb'=4,'x'=4,'y'=4,'zh'=2,'c'=2] {'zb'}, dimensions={0} | all-to-all | bytes 524288 | tf_op jit(solution)/shard_map/all_to_all | solution.py:19
  68.9 0.3 unpack.1
  69.2 15.4 %all-gather = bf16[640,768]{1,0:T(8,128)(2,1)S(1)} all-gather(bf16[160,768]{1,0:T(8,128)(2,1)S(1)} %unpack.1), channel_id=2, replica_groups=mesh['za'=4,'zb'=4,'x'=4,'y'=4,'zh'=2,'c'=2] {'x'}, dimensions={0}, use_global_device_ids=true | all-gather | bytes 1228800 | tf_op jit(solution)/shard_map/all_gather | solution.py:252
  84.6 1.9 %collective-permute-start = (bf16[4,160,768]{2,1,0:T(8,128)(2,1)S(1)}, bf16[4,160,768]{2,1,0:T(8,128)(2,1)S(1)}, u32[]{:S(2)}, u32[]{:S(2)}) collective-permute-start(bf16[4,160,768]{2,1,0:T(8,128)(2,1)S(1)} %bitcast.22), channel_id=1, source_target_pairs={{0,1},{1,0},{2,3},{3,2},{4,5},{5,4},{6,7},{7,6},{8,9},{9,8},{10,11... | collective-permute-start | bytes 2949128 | tf_op jit(solution)/shard_map/ppermute | solution.py:23
  86.5 2.5 %collective-permute-done.rows_ref = bf16[4,160,768]{2,1,0:T(8,128)(2,1)S(1)} collective-permute-done((bf16[4,160,768]{2,1,0:T(8,128)(2,1)S(1)}, bf16[4,160,768]{2,1,0:T(8,128)(2,1)S(1)}, u32[]{:S(2)}, u32[]{:S(2)}) %collective-permute-start) | collective-permute-done | bytes 983072 | tf_op jit(solution)/shard_map/ppermute | solution.py:23
  89.0 0.8 other.1
  89.8 2.0 %collective-permute-start.1 = (bf16[4,160,768]{2,1,0:T(8,128)(2,1)S(1)}, bf16[4,160,768]{2,1,0:T(8,128)(2,1)S(1)}, u32[]{:S(2)}, u32[]{:S(2)}) collective-permute-start(bf16[4,160,768]{2,1,0:T(8,128)(2,1)S(1)} %other.1), channel_id=1, source_target_pairs={{0,1},{1,0},{2,3},{3,2},{4,5},{5,4},{6,7},{7,6},{8,9},{9,8},{10,11... | collective-permute-start | bytes 2949128 | tf_op jit(solution)/shard_map/ppermute | solution.py:23
  91.8 0.8 own.1
  92.6 1.6 %collective-permute-done.1 = bf16[4,160,768]{2,1,0:T(8,128)(2,1)S(1)} collective-permute-done((bf16[4,160,768]{2,1,0:T(8,128)(2,1)S(1)}, bf16[4,160,768]{2,1,0:T(8,128)(2,1)S(1)}, u32[]{:S(2)}, u32[]{:S(2)}) %collective-permute-start.1) | collective-permute-done | bytes 983072 | tf_op jit(solution)/shard_map/ppermute | solution.py:23
  94.2 0.2 add_convert_fusion
  94.5 0.0 copy-start.3
  94.5 18.3 %all_to_all.26.in_ref = bf16[4,160,768]{2,1,0:T(8,128)(2,1)S(1)} all-to-all(bf16[4,160,768]{2,1,0:T(8,128)(2,1)S(1)} %add_convert_fusion), channel_id=1, replica_groups=mesh['za'=4,'zb'=4,'x'=4,'y'=4,'zh'=2,'c'=2] {'x'}, dimensions={0} | all-to-all | bytes 1966080 | tf_op jit(solution)/shard_map/all_to_all | solution.py:19
  112.8 0.4 pack.1
  113.2 9.8 %all_to_all.27 = bf16[4,256,128]{2,1,0:T(8,128)(2,1)S(1)} all-to-all(bf16[4,256,128]{2,1,0:T(8,128)(2,1)S(1)} %bitcast.26), channel_id=1, replica_groups=mesh['za'=4,'zb'=4,'x'=4,'y'=4,'zh'=2,'c'=2] {'zb'}, dimensions={0} | all-to-all | bytes 524288 | tf_op jit(solution)/shard_map/all_to_all | solution.py:19
  123.1 30.8 %all_to_all.28 = bf16[32,8,128]{2,1,0:T(8,128)(2,1)S(1)} all-to-all(bf16[32,8,128]{2,1,0:T(8,128)(2,1)S(1)} %bitcast.34), channel_id=1, replica_groups=mesh['za'=4,'zb'=4,'x'=4,'y'=4,'zh'=2,'c'=2] {'zh','za','y'}, dimensions={0} | all-to-all | bytes 131072 | tf_op jit(solution)/shard_map/all_to_all | solution.py:19
  153.9 0.0 copy-done.3
  153.9 0.9 pick.1
  (4 shorter events, 0.1 us)
Async XLA Ops:
  1.8 56.5 %all-to-all-start = ((bf16[32,8,128]{2,1,0:T(8,128)(2,1)}), bf16[32,8,128]{2,1,0:T(8,128)(2,1)S(1)}, u32[]{:S(2)}, u32[]{:S(2)}) async-start(bf16[32,8,128]{2,1,0:T(8,128)(2,1)} %bitcast.36), calls=%async_computation | async-start | bytes 131072 | tf_op jit(solution)/shard_map/all_to_all | solution.py:19
  33.2 1.1 copy-start
  34.4 1.1 copy-start.1
  35.5 1.1 copy-start.2
  84.6 4.4 %collective-permute-start = (bf16[4,160,768]{2,1,0:T(8,128)(2,1)S(1)}, bf16[4,160,768]{2,1,0:T(8,128)(2,1)S(1)}, u32[]{:S(2)}, u32[]{:S(2)}) collective-permute-start(bf16[4,160,768]{2,1,0:T(8,128)(2,1)S(1)} %bitcast.22), channel_id=1, source_target_pairs={{0,1},{1,0},{2,3},{3,2},{4,5},{5,4},{6,7},{7,6},{8,9},{9,8},{10,11... | collective-permute-start | bytes 2949128 | tf_op jit(solution)/shard_map/ppermute | solution.py:23
  89.8 4.5 %collective-permute-start.1 = (bf16[4,160,768]{2,1,0:T(8,128)(2,1)S(1)}, bf16[4,160,768]{2,1,0:T(8,128)(2,1)S(1)}, u32[]{:S(2)}, u32[]{:S(2)}) collective-permute-start(bf16[4,160,768]{2,1,0:T(8,128)(2,1)S(1)} %other.1), channel_id=1, source_target_pairs={{0,1},{1,0},{2,3},{3,2},{4,5},{5,4},{6,7},{7,6},{8,9},{9,8},{10,11... | collective-permute-start | bytes 2949128 | tf_op jit(solution)/shard_map/ppermute | solution.py:23
  94.5 59.4 %copy-start.3 = (bf16[4,64,64]{2,1,0:T(8,128)(2,1)S(1)}, bf16[4,64,64]{2,1,0:T(8,128)(2,1)}, u32[]{:S(2)}) copy-start(bf16[4,64,64]{2,1,0:T(8,128)(2,1)} %get-tuple-element.34.pick_ref) | copy-start | bytes 98308
